TPU v7x, 16 devices: a whole 2x2x2 slice. The times are simulated.
16 devices in a mesh: fsdp: 16 (over z, y, x, core).
Axes of the slice: x: 2, y: 2, z: 2, core: 2. Of those that a mesh axis runs over, the one named last changes fastest.
Arguments:
- h_in: bfloat16 [32, 1024, 1024], P('fsdp')
- w_gate: bfloat16 [4, 1024, 3072], P(None, 'fsdp')
- w_up: bfloat16 [4, 1024, 3072], P(None, 'fsdp')
- w_down: bfloat16 [4, 3072, 1024], P(None, 'fsdp')
- grad_out: bfloat16 [32, 1024, 1024], P('fsdp')
Outputs:
- output 1: bfloat16 [32, 1024, 1024], P('fsdp')
- output 2: bfloat16 [32, 1024, 1024], P('fsdp')
- output 3: float32 [4, 1024, 3072], P(None, 'fsdp')
- output 4: float32 [4, 1024, 3072], P(None, 'fsdp')
- output 5: float32 [4, 3072, 1024], P(None, 'fsdp')
All inputs are finite; a program needn't handle non-finite values.
Results may differ from a plain program's by a relative error of at most 0.0164932.
Values are sent between devices in bfloat16 or wider.
A program may use at most 1 GiB of HBM per device.

v0:
```python
import jax
import jax.numpy as jnp
from jax import lax
from jax.sharding import PartitionSpec as P, NamedSharding

NORM_EPS = 1e-5


def rms_parts(hidden):
    h_f32 = hidden.astype(jnp.float32)
    inv_rms = lax.rsqrt(jnp.mean(h_f32 * h_f32, axis=-1, keepdims=True) + NORM_EPS)
    return h_f32, inv_rms, (h_f32 * inv_rms).astype(jnp.bfloat16)


def block_fwd(hidden, weights):
    gate_wt, up_wt, down_wt = weights
    h_f32, inv_rms, normed = rms_parts(hidden)
    gate_pre = jnp.einsum("bsd,df->bsf", normed, gate_wt, preferred_element_type=jnp.float32)
    up_pre = jnp.einsum("bsd,df->bsf", normed, up_wt, preferred_element_type=jnp.float32)
    act_out = (gate_pre * jax.nn.sigmoid(gate_pre) * up_pre).astype(jnp.bfloat16)
    return (h_f32 + jnp.einsum("bsf,fd->bsd", act_out, down_wt, preferred_element_type=jnp.float32)).astype(jnp.bfloat16)


def block_bwd(hidden, grad_in, weights):
    gate_wt, up_wt, down_wt = weights
    h_f32, inv_rms, normed = rms_parts(hidden)
    gate_pre = jnp.einsum("bsd,df->bsf", normed, gate_wt, preferred_element_type=jnp.float32)
    up_pre = jnp.einsum("bsd,df->bsf", normed, up_wt, preferred_element_type=jnp.float32)
    sig_gate = jax.nn.sigmoid(gate_pre)
    silu_gate = gate_pre * sig_gate
    act_out = (silu_gate * up_pre).astype(jnp.bfloat16)
    d_act = jnp.einsum("bsd,fd->bsf", grad_in, down_wt, preferred_element_type=jnp.float32)
    d_gate = (d_act * up_pre * (sig_gate * (1.0 + gate_pre * (1.0 - sig_gate)))).astype(jnp.bfloat16)
    d_up = (d_act * silu_gate).astype(jnp.bfloat16)
    d_norm = jnp.einsum("bsf,df->bsd", d_gate, gate_wt, preferred_element_type=jnp.float32) + jnp.einsum("bsf,df->bsd", d_up, up_wt, preferred_element_type=jnp.float32)
    d_hid = inv_rms * d_norm - h_f32 * (inv_rms * inv_rms * inv_rms) * jnp.mean(d_norm * h_f32, axis=-1, keepdims=True)
    new_grad = (grad_in.astype(jnp.float32) + d_hid).astype(jnp.bfloat16)
    layer_grads = (
        jnp.einsum("bsd,bsf->df", normed, d_gate, preferred_element_type=jnp.float32),
        jnp.einsum("bsd,bsf->df", normed, d_up, preferred_element_type=jnp.float32),
        jnp.einsum("bsf,bsd->fd", act_out, grad_in, preferred_element_type=jnp.float32),
    )
    return new_grad, layer_grads


def solution(mesh):
    group_axis = mesh.axis_names[0]
    weight_spec = P(None, group_axis, None)
    token_spec = P(group_axis)

    def gather_layer(stacks, layer_idx):
        return tuple(lax.all_gather(w_stack[layer_idx], group_axis, axis=0, tiled=True) for w_stack in stacks)

    def scatter_grads(layer_grads):
        return tuple(lax.psum_scatter(local_grad, group_axis, scatter_dimension=0, tiled=True) for local_grad in layer_grads)

    def local_step(h_in, w_gate, w_up, w_down, grad_out):
        stacks = (w_gate, w_up, w_down)
        num_layers = w_gate.shape[0]
        keep_count = num_layers // 2
        saved_h = []
        kept_weights = {}
        hidden = h_in
        for layer_idx in range(num_layers):
            full_weights = gather_layer(stacks, layer_idx)
            saved_h.append(hidden)
            hidden = block_fwd(hidden, full_weights)
            if layer_idx >= num_layers - keep_count:
                kept_weights[layer_idx] = full_weights
        grad_in = grad_out
        grad_lists = ([], [], [])
        for layer_idx in reversed(range(num_layers)):
            if layer_idx in kept_weights:
                full_weights = kept_weights[layer_idx]
            else:
                full_weights = gather_layer(stacks, layer_idx)
            grad_in, layer_grads = block_bwd(saved_h[layer_idx], grad_in, full_weights)
            for grad_store, grad_shard in zip(grad_lists, scatter_grads(layer_grads)):
                grad_store.append(grad_shard)
        stacked = tuple(jnp.stack(grad_store[::-1]) for grad_store in grad_lists)
        return hidden, grad_in, stacked[0], stacked[1], stacked[2]

    return jax.shard_map(
        local_step,
        mesh=mesh,
        in_specs=(token_spec, weight_spec, weight_spec, weight_spec, token_spec),
        out_specs=(token_spec, token_spec, weight_spec, weight_spec, weight_spec),
        check_vma=False,
    )
```

profile of v0, /device:TPU:0, one launch (start us, length us, event | category | flops | bytes accessed | tf_op | source)
XLA Modules:
  0.0 1844.3 jit_solution(8325904557958232538)
XLA Ops:
  75.6 25.1 %all-gather.27.cloned.1.call-done = bf16[1,1024,3072]{2,1,0:T(8,128)(2,1)} async-done(((bf16[1,64,3072]{2,1,0:T(8,128)(2,1)}), bf16[1,1024,3072]{2,1,0:T(8,128)(2,1)}) %all-gather.27.cloned.1.call-update) | async-done | bytes 6291472 | tf_op jit(solution)/shard_map/all_gather | solution.py:52
  100.7 33.8 %multiply_convert_fusion.11 = (bf16[2,1024,3072]{2,1,0:T(8,128)(2,1)}, f32[2,1024,3072]{2,1,0:T(8,128)}) fusion(f32[2,1024,3072]{2,1,0:T(8,128)} %fusion.82, bf16[1,1024,3072]{2,1,0:T(8,128)(2,1)} %all-gather.27.cloned.1.call-done, bf16[2,1024,1024]{1,2,0:T(8,128)(2,1)} %copy.39, f32[2,1024]{1,0:T(2,128)S(1)} %get-tuple-element.37), kind=kOutput, calls=%fused_computation.17 | convolution fusion | flops 12928942080 | bytes 73408512 | tf_op jit(solution)/shard_map/bsd,df->bsf/dot_general | solution.py:19
  166.6 23.4 %all-gather.31.cloned.1.call-done = bf16[1,1024,3072]{2,1,0:T(8,128)(2,1)} async-done(((bf16[1,64,3072]{2,1,0:T(8,128)(2,1)}), bf16[1,1024,3072]{2,1,0:T(8,128)(2,1)}) %all-gather.31.cloned.1.call-update) | async-done | bytes 6291472 | tf_op jit(solution)/shard_map/all_gather | solution.py:52
  209.9 24.3 %all-gather.33.cloned.1.call-done = bf16[1,1024,3072]{2,1,0:T(8,128)(2,1)} async-done(((bf16[1,64,3072]{2,1,0:T(8,128)(2,1)}), bf16[1,1024,3072]{2,1,0:T(8,128)(2,1)}) %all-gather.33.cloned.1.call-update) | async-done | bytes 6291472 | tf_op jit(solution)/shard_map/all_gather | solution.py:52
  234.2 33.7 %multiply_convert_fusion.10 = (bf16[2,1024,3072]{2,1,0:T(8,128)(2,1)}, f32[2,1024,3072]{2,1,0:T(8,128)}) fusion(f32[2,1024,3072]{2,1,0:T(8,128)} %fusion.74, bf16[1,1024,3072]{2,1,0:T(8,128)(2,1)} %all-gather.33.cloned.1.call-done, bf16[2,1024,1024]{1,2,0:T(8,128)(2,1)} %get-tuple-element.47, f32[2,1024]{1,0:T(2,128)S(1)} %get-tuple-element.39), kind=kOutput, calls=%fused_computation.14 | convolution fusion | flops 12928942080 | bytes 73408512 | tf_op jit(solution)/shard_map/bsd,df->bsf/dot_general | solution.py:19
  299.9 23.0 %all-gather.37.cloned.1.call-done = bf16[1,1024,3072]{2,1,0:T(8,128)(2,1)} async-done(((bf16[1,64,3072]{2,1,0:T(8,128)(2,1)}), bf16[1,1024,3072]{2,1,0:T(8,128)(2,1)}) %all-gather.37.cloned.1.call-update) | async-done | bytes 6291472 | tf_op jit(solution)/shard_map/all_gather | solution.py:52
  342.8 24.5 %all-gather.39.cloned.1.call-done = bf16[1,1024,3072]{2,1,0:T(8,128)(2,1)} async-done(((bf16[1,64,3072]{2,1,0:T(8,128)(2,1)}), bf16[1,1024,3072]{2,1,0:T(8,128)(2,1)}) %all-gather.39.cloned.1.call-update) | async-done | bytes 6291472 | tf_op jit(solution)/shard_map/all_gather | solution.py:52
  367.3 33.6 %multiply_convert_fusion.9 = (bf16[2,1024,3072]{2,1,0:T(8,128)(2,1)}, f32[2,1024,3072]{2,1,0:T(8,128)}) fusion(f32[2,1024,3072]{2,1,0:T(8,128)} %fusion.66, bf16[1,1024,3072]{2,1,0:T(8,128)(2,1)} %all-gather.39.cloned.1.call-done, bf16[2,1024,1024]{1,2,0:T(8,128)(2,1)} %get-tuple-element.51, f32[2,1024]{1,0:T(2,128)S(1)} %get-tuple-element.41), kind=kOutput, calls=%fused_computation.11 | convolution fusion | flops 12928942080 | bytes 73408512 | tf_op jit(solution)/shard_map/bsd,df->bsf/dot_general | solution.py:19
  432.5 23.5 %all-gather.45.cloned.1.call-done = bf16[1,1024,3072]{2,1,0:T(8,128)(2,1)} async-done(((bf16[1,64,3072]{2,1,0:T(8,128)(2,1)}), bf16[1,1024,3072]{2,1,0:T(8,128)(2,1)}) %all-gather.45.cloned.1.call-update) | async-done | bytes 6291472 | tf_op jit(solution)/shard_map/all_gather | solution.py:52
  475.9 25.0 %all-gather.43.cloned.1.call-done = bf16[1,1024,3072]{2,1,0:T(8,128)(2,1)} async-done(((bf16[1,64,3072]{2,1,0:T(8,128)(2,1)}), bf16[1,1024,3072]{2,1,0:T(8,128)(2,1)}) %all-gather.43.cloned.1.call-update) | async-done | bytes 6291472 | tf_op jit(solution)/shard_map/all_gather | solution.py:52
  521.3 23.9 %all-gather.47.cloned.1.call-done = bf16[1,3072,1024]{2,1,0:T(8,128)(2,1)} async-done(((bf16[1,192,1024]{2,1,0:T(8,128)(2,1)}), bf16[1,3072,1024]{2,1,0:T(8,128)(2,1)}) %all-gather.47.cloned.1.call-update) | async-done | bytes 6291472 | tf_op jit(solution)/shard_map/all_gather | solution.py:52
  545.2 41.5 %multiply_convert_fusion.6 = (bf16[2,1024,3072]{2,1,0:T(8,128)(2,1)}, bf16[2,1024,3072]{2,1,0:T(8,128)(2,1)}, bf16[2,1024,3072]{2,1,0:T(8,128)(2,1)}) fusion(f32[2,1024,3072]{2,1,0:T(8,128)} %fusion.58, f32[2,1024,3072]{2,1,0:T(8,128)} %fusion.54, bf16[2,1024,1024]{2,1,0:T(8,128)(2,1)} %param.9, bf16[1,3072,1024]{2,1,0:T(8,128)(2,1)} %all-gather.47.cloned.1.call-done), kind=kOutput, calls=%fused_computation.6 | convolution fusion | flops 12979273728 | bytes 98566144 | tf_op jit(solution)/shard_map/bsd,fd->bsf/dot_general | solution.py:32
  655.8 41.4 %multiply_convert_fusion.4 = (bf16[2,1024,3072]{2,1,0:T(8,128)(2,1)}, bf16[2,1024,3072]{2,1,0:T(8,128)(2,1)}) fusion(f32[2,1024,3072]{2,1,0:T(8,128)} %fusion.66, f32[2,1024,3072]{2,1,0:T(8,128)} %get-tuple-element.53, bf16[2,1024,1024]{1,2,0:T(8,128)(2,1)} %copy-done.4, bf16[1,3072,1024]{2,1,0:T(8,128)(2,1)} %all-gather.41.cloned.1.call-done), kind=kOutput, calls=%fused_computation.4 | convolution fusion | flops 12966690816 | bytes 85983232 | tf_op jit(solution)/shard_map/bsd,fd->bsf/dot_general | solution.py:32
  716.7 23.1 %fusion.27 = (f32[2,1024]{1,0:T(2,128)S(1)}, f32[2,1024,1024]{1,2,0:T(8,128)}) fusion(bf16[2,1024,1024]{1,2,0:T(8,128)(2,1)S(1)} %copy-done.10, f32[2,1024,1024]{1,2,0:T(8,128)} %fusion.60, bf16[2,1024,3072]{2,1,0:T(8,128)(2,1)} %get-tuple-element.20, bf16[1,1024,3072]{2,1,0:T(8,128)(2,1)} %all-gather.37.cloned.1.call-done), kind=kOutput, calls=%fused_computation.63 | convolution fusion | flops 12893288448 | bytes 39854080 | tf_op jit(solution)/shard_map/bsf,df->bsd/dot_general | solution.py:35
  767.9 41.7 %multiply_convert_fusion.2 = (bf16[2,1024,3072]{2,1,0:T(8,128)(2,1)}, bf16[2,1024,3072]{2,1,0:T(8,128)(2,1)}) fusion(f32[2,1024,3072]{2,1,0:T(8,128)} %fusion.74, f32[2,1024,3072]{2,1,0:T(8,128)} %get-tuple-element.49, bf16[2,1024,1024]{1,2,0:T(8,128)(2,1)} %copy-done.6, bf16[1,3072,1024]{2,1,0:T(8,128)(2,1)} %all-gather.35.cloned.1.call-done), kind=kOutput, calls=%fused_computation.2 | convolution fusion | flops 12966690816 | bytes 85983232 | tf_op jit(solution)/shard_map/bsd,fd->bsf/dot_general | solution.py:32
  829.0 22.8 %fusion.19 = (f32[2,1024]{1,0:T(2,128)S(1)}, f32[2,1024,1024]{1,2,0:T(8,128)}) fusion(bf16[2,1024,1024]{1,2,0:T(8,128)(2,1)S(1)} %copy-done.9, f32[2,1024,1024]{1,2,0:T(8,128)} %fusion.68, bf16[2,1024,3072]{2,1,0:T(8,128)(2,1)} %get-tuple-element.18, bf16[1,1024,3072]{2,1,0:T(8,128)(2,1)} %all-gather.31.cloned.1.call-done), kind=kOutput, calls=%fused_computation.55 | convolution fusion | flops 12893288448 | bytes 39854080 | tf_op jit(solution)/shard_map/bsf,df->bsd/dot_general | solution.py:35
  960.2 40.1 %multiply_convert_fusion = (bf16[2,1024,3072]{2,1,0:T(8,128)(2,1)}, bf16[2,1024,3072]{2,1,0:T(8,128)(2,1)}) fusion(f32[2,1024,3072]{2,1,0:T(8,128)} %fusion.82, f32[2,1024,3072]{2,1,0:T(8,128)} %get-tuple-element.45, bf16[2,1024,1024]{1,2,0:T(8,128)(2,1)} %copy-done.2, bf16[1,3072,1024]{2,1,0:T(8,128)(2,1)} %all-gather.29.cloned.1.call-done), kind=kOutput, calls=%fused_computation | convolution fusion | flops 12966690816 | bytes 85983232 | tf_op jit(solution)/shard_map/bsd,fd->bsf/dot_general | solution.py:32
  1187.7 70.8 %reduce-scatter.25.cloned.1.call-done = f32[64,3072]{1,0:T(8,128)} async-done(((f32[1024,3072]{1,0:T(8,128)}), f32[64,3072]{1,0:T(8,128)}) %reduce-scatter.25.cloned.1.call-update) | async-done | bytes 786448 | tf_op jit(solution)/shard_map/reduce_scatter | solution.py:55
  1258.5 95.9 %reduce-scatter.27.cloned.1.call-done = f32[64,3072]{1,0:T(8,128)} async-done(((f32[1024,3072]{1,0:T(8,128)}), f32[64,3072]{1,0:T(8,128)}) %reduce-scatter.27.cloned.1.call-update) | async-done | bytes 786448 | tf_op jit(solution)/shard_map/reduce_scatter | solution.py:55
  1354.4 95.7 %reduce-scatter.21.cloned.1.call-done = f32[64,3072]{1,0:T(8,128)} async-done(((f32[1024,3072]{1,0:T(8,128)}), f32[64,3072]{1,0:T(8,128)}) %reduce-scatter.21.cloned.1.call-update) | async-done | bytes 786448 | tf_op jit(solution)/shard_map/reduce_scatter | solution.py:55
  1453.9 92.0 %reduce-scatter.15.cloned.1.call-done = f32[64,3072]{1,0:T(8,128)} async-done(((f32[1024,3072]{1,0:T(8,128)}), f32[64,3072]{1,0:T(8,128)}) %reduce-scatter.15.cloned.1.call-update) | async-done | bytes 786448 | tf_op jit(solution)/shard_map/reduce_scatter | solution.py:55
  1546.0 95.9 %reduce-scatter.17.cloned.1.call-done = f32[64,3072]{1,0:T(8,128)} async-done(((f32[1024,3072]{1,0:T(8,128)}), f32[64,3072]{1,0:T(8,128)}) %reduce-scatter.17.cloned.1.call-update) | async-done | bytes 786448 | tf_op jit(solution)/shard_map/reduce_scatter | solution.py:55
  1641.8 95.9 %reduce-scatter.19.cloned.1.call-done = f32[64,3072]{1,0:T(8,128)} async-done(((f32[1024,3072]{1,0:T(8,128)}), f32[64,3072]{1,0:T(8,128)}) %reduce-scatter.19.cloned.1.call-update) | async-done | bytes 786448 | tf_op jit(solution)/shard_map/reduce_scatter | solution.py:55
  1737.7 95.7 %reduce-scatter.13.cloned.1.call-done = f32[64,3072]{1,0:T(8,128)} async-done(((f32[1024,3072]{1,0:T(8,128)}), f32[64,3072]{1,0:T(8,128)}) %reduce-scatter.13.cloned.1.call-update) | async-done | bytes 786448 | tf_op jit(solution)/shard_map/reduce_scatter | solution.py:55
  (159 shorter events, 683.3 us)
Async XLA Ops:
  7.2 48.6 %all-gather.25.cloned.1.call-start = ((), (), s32[]{:S(2)}) async-start(), calls=%async_computation.24 | async-start | bytes 6684672 | tf_op jit(solution)/shard_map/all_gather | solution.py:52
  9.8 90.9 %all-gather.27.cloned.1.call-start = ((), (), s32[]{:S(2)}) async-start(), calls=%async_computation.25 | async-start | bytes 6684672 | tf_op jit(solution)/shard_map/all_gather | solution.py:52
  12.4 132.7 %all-gather.29.cloned.1.call-start = ((), (), s32[]{:S(2)}) async-start(), calls=%async_computation.26 | async-start | bytes 6684672 | tf_op jit(solution)/shard_map/all_gather | solution.py:52
  15.0 174.9 %all-gather.31.cloned.1.call-start = ((), (), s32[]{:S(2)}) async-start(), calls=%async_computation.27 | async-start | bytes 6684672 | tf_op jit(solution)/shard_map/all_gather | solution.py:52
  15.6 218.6 %all-gather.33.cloned.1.call-start = ((), (), s32[]{:S(2)}) async-start(), calls=%async_computation.28 | async-start | bytes 6684672 | tf_op jit(solution)/shard_map/all_gather | solution.py:52
  16.2 262.3 %all-gather.35.cloned.1.call-start = ((), (), s32[]{:S(2)}) async-start(), calls=%async_computation.29 | async-start | bytes 6684672 | tf_op jit(solution)/shard_map/all_gather | solution.py:52
  16.8 306.1 %all-gather.37.cloned.1.call-start = ((), (), s32[]{:S(2)}) async-start(), calls=%async_computation.30 | async-start | bytes 6684672 | tf_op jit(solution)/shard_map/all_gather | solution.py:52
  17.5 349.7 %all-gather.39.cloned.1.call-start = ((), (), s32[]{:S(2)}) async-start(), calls=%async_computation.31 | async-start | bytes 6684672 | tf_op jit(solution)/shard_map/all_gather | solution.py:52
  18.3 393.4 %all-gather.41.cloned.1.call-start = ((), (), s32[]{:S(2)}) async-start(), calls=%async_computation.32 | async-start | bytes 6684672 | tf_op jit(solution)/shard_map/all_gather | solution.py:52
  19.0 436.9 %all-gather.45.cloned.1.call-start = ((), (), s32[]{:S(2)}) async-start(), calls=%async_computation.34 | async-start | bytes 6684672 | tf_op jit(solution)/shard_map/all_gather | solution.py:52
  19.6 481.3 %all-gather.43.cloned.1.call-start = ((), (), s32[]{:S(2)}) async-start(), calls=%async_computation.33 | async-start | bytes 6684672 | tf_op jit(solution)/shard_map/all_gather | solution.py:52
  20.3 524.8 %all-gather.47.cloned.1.call-start = ((), (), s32[]{:S(2)}) async-start(), calls=%async_computation.35 | async-start | bytes 6684672 | tf_op jit(solution)/shard_map/all_gather | solution.py:52
  20.9 1162.5 %reduce-scatter.33.cloned.1.call-start = ((), (), s32[]{:S(2)}) async-start(), calls=%async_computation.22 | async-start | bytes 13369344 | tf_op jit(solution)/shard_map/reduce_scatter | solution.py:55
  655.7 527.7 %reduce-scatter.31.cloned.1.call-start = ((), (), s32[]{:S(2)}) async-start(), calls=%async_computation.21 | async-start | bytes 13369344 | tf_op jit(solution)/shard_map/reduce_scatter | solution.py:55
  767.8 415.6 %reduce-scatter.29.cloned.1.call-start = ((), (), s32[]{:S(2)}) async-start(), calls=%async_computation.20 | async-start | bytes 13369344 | tf_op jit(solution)/shard_map/reduce_scatter | solution.py:55
  879.8 303.6 %reduce-scatter.35.cloned.1.call-start = ((), (), s32[]{:S(2)}) async-start(), calls=%async_computation.23 | async-start | bytes 13369344 | tf_op jit(solution)/shard_map/reduce_scatter | solution.py:55
  899.7 288.0 %reduce-scatter.23.cloned.1.call-start = ((), (), s32[]{:S(2)}) async-start(), calls=%async_computation.17 | async-start | bytes 13369344 | tf_op jit(solution)/shard_map/reduce_scatter | solution.py:55
  919.7 338.7 %reduce-scatter.25.cloned.1.call-start = ((), (), s32[]{:S(2)}) async-start(), calls=%async_computation.18 | async-start | bytes 13369344 | tf_op jit(solution)/shard_map/reduce_scatter | solution.py:55
  939.9 414.5 %reduce-scatter.27.cloned.1.call-start = ((), (), s32[]{:S(2)}) async-start(), calls=%async_computation.19 | async-start | bytes 13369344 | tf_op jit(solution)/shard_map/reduce_scatter | solution.py:55
  960.2 489.9 %reduce-scatter.21.cloned.1.call-start = ((), (), s32[]{:S(2)}) async-start(), calls=%async_computation.16 | async-start | bytes 13369344 | tf_op jit(solution)/shard_map/reduce_scatter | solution.py:55
  1019.6 526.4 %reduce-scatter.15.cloned.1.call-start = ((), (), s32[]{:S(2)}) async-start(), calls=%async_computation.13 | async-start | bytes 13369344 | tf_op jit(solution)/shard_map/reduce_scatter | solution.py:55
  1039.7 602.2 %reduce-scatter.17.cloned.1.call-start = ((), (), s32[]{:S(2)}) async-start(), calls=%async_computation.14 | async-start | bytes 13369344 | tf_op jit(solution)/shard_map/reduce_scatter | solution.py:55
  1059.4 678.3 %reduce-scatter.19.cloned.1.call-start = ((), (), s32[]{:S(2)}) async-start(), calls=%async_computation.15 | async-start | bytes 13369344 | tf_op jit(solution)/shard_map/reduce_scatter | solution.py:55
  1079.1 754.4 %reduce-scatter.13.cloned.1.call-start = ((), (), s32[]{:S(2)}) async-start(), calls=%async_computation.12 | async-start | bytes 13369344 | tf_op jit(solution)/shard_map/reduce_scatter | solution.py:55
  (26 other events, 730.4 us)
Sparse Core Ops, SparseCore 0:
  10.8 44.9 all-gather.24
  58.5 42.1 all-gather.26
  103.0 42.1 all-gather.28
  147.8 42.1 all-gather.30
  192.0 42.1 all-gather.32
  236.3 42.1 all-gather.34
  280.7 42.1 all-gather.36
  325.1 42.1 all-gather.38
  369.5 42.1 all-gather.40
  413.8 42.1 all-gather.44
  458.8 42.1 all-gather.42
  503.0 42.1 all-gather.46
  655.8 91.2 reduce-scatter.32
  767.9 91.0 reduce-scatter.30
  880.0 91.2 reduce-scatter.28
  975.7 91.2 reduce-scatter.34
  1071.5 91.2 reduce-scatter.22
  1167.2 91.2 reduce-scatter.24
  1263.1 91.2 reduce-scatter.26
  1358.8 91.2 reduce-scatter.20
  1454.7 91.2 reduce-scatter.14
  1550.6 91.2 reduce-scatter.16
  1646.5 91.2 reduce-scatter.18
  1742.2 91.2 reduce-scatter.12
where the time goes:
time: 1850 us; the launch traced here: 1840 us
  waiting for transfers between devices  890 us (48%)
  matrix products  845 us (46%)
  other arithmetic  50.6 us (3%)
  local copies, waits for them, and re-layouts  41.8 us (2%)
    reduce_scatter x12, waiting for transfers between devices, scatter_grads(): lax.psum_scatter(local_grad, group_axis, scatter_dimension=0, tiled=True)  642 us
    all_gather x12, waiting for transfers between devices, gather_layer(): lax.all_gather(w_stack[layer_idx], group_axis, axis=0, tiled=True)  243 us
    dot_general x4, matrix products, block_bwd(): jnp.einsum('bsd,fd->bsf', grad_in, down_wt, preferred_element_type=jnp.fl...  165 us
    dot_general x4, matrix products, block_fwd(): jnp.einsum('bsd,df->bsf', normed, up_wt, preferred_element_type=jnp.float32)  121 us
    dot_general x4, matrix products, block_bwd(): jnp.einsum('bsf,df->bsd', d_gate, gate_wt, preferred_element_type=jnp.flo...  89.5 us
    dot_general x4, matrix products, block_fwd(): jnp.einsum('bsf,fd->bsd', act_out, down_wt, preferred_element_type=jnp.fl...  82.6 us
    dot_general x4, matrix products, block_fwd(): jnp.einsum('bsd,df->bsf', normed, gate_wt, preferred_element_type=jnp.flo...  80.2 us
    dot_general x4, matrix products, block_bwd(): jnp.einsum('bsd,bsf->df', normed, d_up, preferred_element_type=jnp.float32)  78.2 us
  transfers between devices with their start and end apart: 24, of which 19 were waited for; matrix products, arithmetic and copies ran while one was open for 44% of the time, Pallas kernels for 0%

commit v1 on v0

v1 whole, which is shorter than its diff:
```python
import functools

import jax
import jax.numpy as jnp
from jax import lax
from jax.experimental import pallas as pl
from jax.experimental.pallas import tpu as pltpu
from jax.sharding import PartitionSpec as P


NORM_EPS = 1e-5
CORE, X, Y, Z = 1, 2, 4, 8
AXIS_BITS = (X, Y, Z)
TM = 1024
TF = 768
SUB_FWD, SUB_BWD = 2, 4
TD = 512
VMEM_BYTES = 60 * 1024 * 1024
FLIGHT, T_DOWN, T_BWD, T_IN = 95.0, 21.0, 66.0, 20.0


def params(semantics):
    return pltpu.CompilerParams(dimension_semantics=semantics, vmem_limit_bytes=VMEM_BYTES)


def t_dot(lhs, rhs):
    return lax.dot_general(lhs, rhs, (((0,), (0,)), ((), ())), preferred_element_type=jnp.float32)


MESH_ID = pl.DeviceIdType.MESH
GATHER_STEPS = (0, 2, 5, 7)


class Gather:
    def __init__(self, axis, shards, fulls, sends, recvs, locals_):
        self.shards, self.fulls = shards, fulls
        self.sends, self.recvs, self.locals_ = sends, recvs, locals_
        me = lax.axis_index(axis)
        self.core = me % 2
        self.coord = {Z: me // 8, Y: (me // 4) % 2, X: (me // 2) % 2}
        self.partner = {
            CORE: me + 1 - 2 * self.core,
            X: me + 2 - 4 * self.coord[X],
            Y: me + 4 - 8 * self.coord[Y],
            Z: me + 8 - 16 * self.coord[Z],
        }

    def order(self, k):
        return tuple(AXIS_BITS[(k + i) % 3] for i in range(3))

    def piece(self, k, free=(), flipped=None):
        index = []
        for bit in (Z, Y, X):
            if bit in free:
                index.append(slice(None))
            elif bit == flipped:
                index.append(1 - self.coord[bit])
            else:
                index.append(self.coord[bit])
        return self.fulls[k].at[tuple(index) + (self.core,)]

    def remote(self, k, slot, src, dst, bit):
        return pltpu.make_async_remote_copy(
            src_ref=src,
            dst_ref=dst,
            send_sem=self.sends.at[k, slot],
            recv_sem=self.recvs.at[k, slot],
            device_id=(self.partner[bit],),
            device_id_type=MESH_ID,
        )

    def along(self, k, s, j):
        if j == 0:
            return self.remote(k, (0, 1, 3)[s], self.shards[k], self.piece(k), self.order(k)[s])
        part = self.piece(k, self.order(k)[: j - 1], self.order(k)[j - 1])
        return self.remote(k, (0, 1, 3)[s] + j, part, part, self.order(k)[s])

    def arrived(self, k, s, j):
        return self.along(k, s, j)

    def across(self, k, s, j):
        if s < 0:
            return self.remote(k, 6, self.shards[k], self.piece(k), CORE)
        order = self.order(k)
        free = order[: j - 1] if j > 0 else ()
        index = []
        for bit in (Z, Y, X):
            if bit in free:
                index.append(slice(None))
            elif bit == order[s] or (j > 0 and bit == order[j - 1]):
                index.append(1 - self.coord[bit])
            else:
                index.append(self.coord[bit])
        part = self.fulls[k].at[tuple(index) + (self.core,)]
        return self.remote(k, 7 + (0, 1, 3)[s] + j, part, part, CORE)

    def own(self, k):
        return pltpu.make_async_copy(self.shards[k], self.piece(k), self.locals_.at[k])

    def begin(self):
        barrier = pltpu.get_barrier_semaphore()
        for bit in (CORE, X, Y, Z):
            pl.semaphore_signal(barrier, inc=1, device_id=(self.partner[bit],), device_id_type=MESH_ID)
        pl.semaphore_wait(barrier, 4)
        for s in range(3):
            for k in range(3):
                self.along(k, s, 0).start()
        for k in range(3):
            self.across(k, -1, 0).start()
            self.own(k).start()

    def take(self, k, s, j):
        self.arrived(k, s, j).wait_recv()
        self.across(k, s, j).start()

    def advance(self, s):
        for k in range(3):
            if s == 1:
                self.take(k, 0, 0)
                self.along(k, 1, 1).start()
                self.along(k, 2, 1).start()
            elif s == 2:
                self.take(k, 1, 0)
                self.take(k, 1, 1)
                self.along(k, 2, 2).start()
            else:
                self.take(k, 2, 0)
                self.take(k, 2, 1)

    def finish(self):
        for k in range(3):
            self.take(k, 2, 2)
        for k in range(3):
            self.own(k).wait()
            for s in range(3):
                for j in range(s + 1):
                    self.along(k, s, j).wait_send()
                    self.across(k, s, j).wait()
            self.across(k, -1, 0).wait()


GATHER_SCRATCH = [
    pltpu.SemaphoreType.DMA((3, 13)),
    pltpu.SemaphoreType.DMA((3, 13)),
    pltpu.SemaphoreType.DMA((3,)),
]
ANY = pl.BlockSpec(memory_space=pl.ANY)


def full_shapes(shards):
    return [jax.ShapeDtypeStruct((2, 2, 2, 2) + w.shape, w.dtype) for w in shards]


def flat(fulls):
    return tuple(w.reshape(-1, w.shape[-1]) for w in fulls)


def gather_first(axis, shards):
    def kernel(*refs):
        gather = Gather(axis, refs[:3], refs[3:6], *refs[6:9])
        gather.begin()
        for s in (1, 2, 3):
            gather.advance(s)
        gather.finish()

    return flat(
        pl.pallas_call(
            kernel,
            in_specs=[ANY] * 3,
            out_specs=[ANY] * 3,
            out_shape=full_shapes(shards),
            scratch_shapes=GATHER_SCRATCH,
            compiler_params=pltpu.CompilerParams(collective_id=0, has_side_effects=True),
            name="gather_first",
        )(*shards)
    )


def fwd_gather_kernel(axis, *refs):
    main, shards, outs, fulls, scratch, sems = refs[:4], refs[4:7], refs[7:12], refs[12:15], refs[15:17], refs[17:]
    step = pl.program_id(0) * pl.num_programs(1) + pl.program_id(1)
    gather = Gather(axis, shards, fulls, *sems)
    pl.when(step == GATHER_STEPS[0])(gather.begin)
    for s in (1, 2, 3):
        pl.when(step == GATHER_STEPS[s])(functools.partial(gather.advance, s))
    fwd_kernel(*main, *outs, *scratch)
    pl.when(step == pl.num_programs(0) * pl.num_programs(1) - 1)(gather.finish)


def fwd_kernel(h_ref, wg_ref, wu_ref, wd_ref, out_ref, n_ref, gate_ref, up_ref, act_ref, n_all, acc):
    f, m = pl.program_id(0), pl.program_id(1)
    rows = pl.ds(pl.multiple_of(m * TM, TM), TM)

    @pl.when(f == 0)
    def _():
        h_f32 = h_ref[...].astype(jnp.float32)
        inv_rms = lax.rsqrt(jnp.mean(h_f32 * h_f32, axis=-1, keepdims=True) + NORM_EPS)
        normed = (h_f32 * inv_rms).astype(jnp.bfloat16)
        n_all[rows, :] = normed
        n_ref[...] = normed

    @pl.when(f == 0)
    def _():
        acc[rows, :] = jnp.zeros((TM, acc.shape[1]), jnp.float32)

    for sub in range(SUB_FWD):
        size = TM // SUB_FWD
        here = pl.ds(sub * size, size)
        there = pl.ds(pl.multiple_of(m * TM + sub * size, size), size)
        normed = n_all[there, :]
        gate = jnp.dot(normed, wg_ref[...], preferred_element_type=jnp.float32)
        up = jnp.dot(normed, wu_ref[...], preferred_element_type=jnp.float32)
        gate_ref[here, :] = gate
        up_ref[here, :] = up
        act = (gate * jax.nn.sigmoid(gate) * up).astype(jnp.bfloat16)
        act_ref[here, :] = act
        acc[there, :] += jnp.dot(act, wd_ref[...], preferred_element_type=jnp.float32)

    @pl.when(f == pl.num_programs(0) - 1)
    def _():
        out_ref[...] = (h_ref[...].astype(jnp.float32) + acc[rows, :]).astype(jnp.bfloat16)


def fwd_layer(axis, hidden, wg, wu, wd, shards=()):
    tokens, width = hidden.shape
    ff = wg.shape[1]
    nf, nm = ff // TF, tokens // TM
    more = len(shards)
    result = pl.pallas_call(
        functools.partial(fwd_gather_kernel, axis) if more else fwd_kernel,
        grid=(nf, nm),
        in_specs=[
            pl.BlockSpec((TM, width), lambda f, m: (m, 0)),
            pl.BlockSpec((width, TF), lambda f, m: (0, f)),
            pl.BlockSpec((width, TF), lambda f, m: (0, f)),
            pl.BlockSpec((TF, width), lambda f, m: (f, 0)),
        ]
        + [ANY] * more,
        out_specs=[
            pl.BlockSpec((TM, width), lambda f, m: (jnp.where(f == nf - 1, m, 0), 0)),
            pl.BlockSpec((TM, width), lambda f, m: (jnp.where(f == 0, m, nm - 1), 0)),
            pl.BlockSpec((TM, TF), lambda f, m: (m, f)),
            pl.BlockSpec((TM, TF), lambda f, m: (m, f)),
            pl.BlockSpec((TM, TF), lambda f, m: (m, f)),
        ]
        + [ANY] * more,
        out_shape=[
            jax.ShapeDtypeStruct((tokens, width), jnp.bfloat16),
            jax.ShapeDtypeStruct((tokens, width), jnp.bfloat16),
            jax.ShapeDtypeStruct((tokens, ff), jnp.float32),
            jax.ShapeDtypeStruct((tokens, ff), jnp.float32),
            jax.ShapeDtypeStruct((tokens, ff), jnp.bfloat16),
        ]
        + full_shapes(shards),
        scratch_shapes=[pltpu.VMEM((tokens, width), jnp.bfloat16), pltpu.VMEM((tokens, width), jnp.float32)]
        + (GATHER_SCRATCH if more else []),
        compiler_params=pltpu.CompilerParams(
            dimension_semantics=("arbitrary", "arbitrary"),
            vmem_limit_bytes=VMEM_BYTES,
            **(dict(collective_id=1, has_side_effects=True) if more else {}),
        ),
        cost_estimate=pl.CostEstimate(flops=6 * tokens * width * ff, bytes_accessed=12 * tokens * ff, transcendentals=0),
        name="fwd_gather" if more else "fwd_layer",
    )(hidden, wg, wu, wd, *shards)
    return result[:5], flat(result[5:])


def bwd_kernel(h_ref, g_ref, gate_ref, up_ref, wg_ref, wu_ref, wd_ref, out_ref, dgate_ref, dup_ref, acc, wg_t, wu_t, wd_t):
    f, m = pl.program_id(0), pl.program_id(1)
    rows = pl.ds(pl.multiple_of(m * TM, TM), TM)

    @pl.when(m == 0)
    def _():
        wd_t[...] = wd_ref[...].T
        wg_t[...] = wg_ref[...].T
        wu_t[...] = wu_ref[...].T

    @pl.when(f == 0)
    def _():
        acc[rows, :] = jnp.zeros((TM, acc.shape[1]), jnp.float32)

    for sub in range(SUB_BWD):
        size = TM // SUB_BWD
        here = pl.ds(sub * size, size)
        there = pl.ds(pl.multiple_of(m * TM + sub * size, size), size)
        d_act = jnp.dot(g_ref[here, :], wd_t[...], preferred_element_type=jnp.float32)
        gate, up = gate_ref[here, :], up_ref[here, :]
        sig = jax.nn.sigmoid(gate)
        d_gate = (d_act * up * (sig * (1.0 + gate * (1.0 - sig)))).astype(jnp.bfloat16)
        d_up = (d_act * (gate * sig)).astype(jnp.bfloat16)
        dgate_ref[here, :] = d_gate
        dup_ref[here, :] = d_up
        acc[there, :] += jnp.dot(d_gate, wg_t[...], preferred_element_type=jnp.float32) + jnp.dot(
            d_up, wu_t[...], preferred_element_type=jnp.float32
        )

    @pl.when(f == pl.num_programs(0) - 1)
    def _():
        h_f32 = h_ref[...].astype(jnp.float32)
        inv_rms = lax.rsqrt(jnp.mean(h_f32 * h_f32, axis=-1, keepdims=True) + NORM_EPS)
        d_norm = acc[rows, :]
        d_hid = inv_rms * d_norm - h_f32 * (inv_rms * inv_rms * inv_rms) * jnp.mean(d_norm * h_f32, axis=-1, keepdims=True)
        out_ref[...] = (g_ref[...].astype(jnp.float32) + d_hid).astype(jnp.bfloat16)


def bwd_layer(hidden, grad_in, gate, up, wg, wu, wd):
    tokens, width = hidden.shape
    ff = wg.shape[1]
    nf, nm = ff // TF, tokens // TM
    return pl.pallas_call(
        bwd_kernel,
        grid=(nf, nm),
        in_specs=[
            pl.BlockSpec((TM, width), lambda f, m: (jnp.where(f == nf - 1, m, 0), 0)),
            pl.BlockSpec((TM, width), lambda f, m: (m, 0)),
            pl.BlockSpec((TM, TF), lambda f, m: (m, f)),
            pl.BlockSpec((TM, TF), lambda f, m: (m, f)),
            pl.BlockSpec((width, TF), lambda f, m: (0, f)),
            pl.BlockSpec((width, TF), lambda f, m: (0, f)),
            pl.BlockSpec((TF, width), lambda f, m: (f, 0)),
        ],
        out_specs=[
            pl.BlockSpec((TM, width), lambda f, m: (jnp.where(f == nf - 1, m, 0), 0)),
            pl.BlockSpec((TM, TF), lambda f, m: (m, f)),
            pl.BlockSpec((TM, TF), lambda f, m: (m, f)),
        ],
        out_shape=[
            jax.ShapeDtypeStruct((tokens, width), jnp.bfloat16),
            jax.ShapeDtypeStruct((tokens, ff), jnp.bfloat16),
            jax.ShapeDtypeStruct((tokens, ff), jnp.bfloat16),
        ],
        scratch_shapes=[
            pltpu.VMEM((tokens, width), jnp.float32),
            pltpu.VMEM((TF, width), jnp.bfloat16),
            pltpu.VMEM((TF, width), jnp.bfloat16),
            pltpu.VMEM((width, TF), jnp.bfloat16),
        ],
        compiler_params=params(("arbitrary", "arbitrary")),
        cost_estimate=pl.CostEstimate(flops=6 * tokens * width * ff, bytes_accessed=12 * tokens * ff, transcendentals=0),
        name="bwd_layer",
    )(hidden, grad_in, gate, up, wg, wu, wd)


def dw_in_kernel(n_ref, d_ref, out_ref):
    out_ref[...] = t_dot(n_ref[...], d_ref[...])


def dw_in(normed, d_hidden):
    tokens, width = normed.shape
    ff = d_hidden.shape[1]
    return pl.pallas_call(
        dw_in_kernel,
        grid=(ff // TD,),
        in_specs=[pl.BlockSpec((tokens, width), lambda f: (0, 0)), pl.BlockSpec((tokens, TD), lambda f: (0, f))],
        out_specs=pl.BlockSpec((width, TD), lambda f: (0, f)),
        out_shape=jax.ShapeDtypeStruct((width, ff), jnp.float32),
        compiler_params=params(("arbitrary",)),
        cost_estimate=pl.CostEstimate(flops=2 * tokens * width * ff, bytes_accessed=4 * width * ff, transcendentals=0),
        name="dw_in",
    )(normed, d_hidden)


def dw_in_split_kernel(block_of, n_ref, d_ref, keep_ref, send_ref, full):
    shard = keep_ref.shape[1]
    full[...] = t_dot(n_ref[...], d_ref[...])
    core = block_of[8]
    for q in range(8):
        base = block_of[q] * (2 * shard)
        keep_ref[q] = full[pl.ds(pl.multiple_of(base + core * shard, shard), shard), :]
        send_ref[q] = full[pl.ds(pl.multiple_of(base + (1 - core) * shard, shard), shard), :]


def dw_in_split(block_of, normed, d_hidden, first, cols):
    tokens, width = normed.shape
    tile = TD
    shard = width // 16
    out = jax.ShapeDtypeStruct((8, shard, cols), jnp.float32)
    return pl.pallas_call(
        dw_in_split_kernel,
        grid_spec=pltpu.PrefetchScalarGridSpec(
            num_scalar_prefetch=1,
            grid=(cols // tile,),
            in_specs=[
                pl.BlockSpec((tokens, width), lambda f, t: (0, 0)),
                pl.BlockSpec((tokens, tile), lambda f, t: (0, first // tile + f)),
            ],
            out_specs=[pl.BlockSpec((8, shard, tile), lambda f, t: (0, 0, f))] * 2,
            scratch_shapes=[pltpu.VMEM((width, tile), jnp.float32)],
        ),
        out_shape=[out, out],
        compiler_params=params(("arbitrary",)),
        cost_estimate=pl.CostEstimate(flops=2 * tokens * width * cols, bytes_accessed=4 * width * cols, transcendentals=0),
        name="dw_in_split",
    )(block_of, normed, d_hidden)


def dw_down_split_kernel(block_of, act_ref, g_ref, keep_ref, send_ref, full):
    shard = keep_ref.shape[1]
    full[...] = t_dot(act_ref[...], g_ref[...])
    core = block_of[8]
    keep_ref[0] = full[pl.ds(pl.multiple_of(core * shard, shard), shard), :]
    send_ref[0] = full[pl.ds(pl.multiple_of((1 - core) * shard, shard), shard), :]


def dw_down_split(block_of, act, grad_in):
    tokens, ff = act.shape
    width = grad_in.shape[1]
    shard = ff // 16
    out = jax.ShapeDtypeStruct((8, shard, width), jnp.float32)
    return pl.pallas_call(
        dw_down_split_kernel,
        grid_spec=pltpu.PrefetchScalarGridSpec(
            num_scalar_prefetch=1,
            grid=(8,),
            in_specs=[
                pl.BlockSpec((tokens, 2 * shard), lambda q, t: (0, t[q])),
                pl.BlockSpec((tokens, width), lambda q, t: (0, 0)),
            ],
            out_specs=[pl.BlockSpec((1, shard, width), lambda q, t: (q, 0, 0))] * 2,
            scratch_shapes=[pltpu.VMEM((2 * shard, width), jnp.float32)],
        ),
        out_shape=[out, out],
        compiler_params=params(("arbitrary",)),
        cost_estimate=pl.CostEstimate(flops=2 * tokens * width * ff, bytes_accessed=4 * width * ff, transcendentals=0),
        name="dw_down_split",
    )(block_of, act, grad_in)


def solution(mesh):
    group_axis = mesh.axis_names[0]
    size = mesh.shape[group_axis]
    weight_spec = P(None, group_axis, None)
    token_spec = P(group_axis)

    def swap(value, bit):
        return lax.ppermute(value, group_axis, [(i, i ^ bit) for i in range(size)])

    def chip_table(order):
        me = lax.axis_index(group_axis).astype(jnp.int32)
        entries = []
        for q in range(8):
            bits = sum(bit for i, bit in enumerate(order) if (q >> (2 - i)) & 1)
            entries.append((me ^ bits) >> 1)
        return jnp.stack(entries + [me & 1])

    def fence(value, anchors):
        return lax.optimization_barrier((value,) + tuple(anchors))[0]

    class Chain:
        def __init__(self, keep, send, order, now):
            self.keep, self.bits, self.got = keep, (CORE,) + order, []
            self.result = None
            self.unit = FLIGHT * keep.size / (8 * 64 * 3072)
            self.launch(send, now)

        def launch(self, part, now):
            stage = len(self.got)
            self.flying = swap(part, self.bits[stage])
            self.ready = now + 2.0 + self.unit * (0.15, 1.0, 0.5, 0.25)[stage]

        def step(self, anchors, now):
            self.got.append(fence(self.flying, anchors))
            low, high = ((4, 8), (2, 4), (1, 2), (0, 1))[len(self.got) - 1]
            total = self.keep[low:high]
            for arrived in self.got:
                total = total + arrived[low:high]
            if low == 0:
                self.result, self.ready = total[0], None
            else:
                self.launch(total, now)
            return total

    def local_step(h_in, w_gate, w_up, w_down, grad_out):
        stacks = (w_gate, w_up, w_down)
        num_layers = w_gate.shape[0]
        shape = h_in.shape
        hidden = h_in.reshape(-1, shape[-1])
        grad_in = grad_out.reshape(-1, shape[-1])
        shards = [tuple(w[layer] for w in stacks) for layer in range(num_layers)]
        saved = []
        weights = gather_first(group_axis, shards[0])
        for layer in range(num_layers):
            following = shards[layer + 1] if layer + 1 < num_layers else ()
            (out, normed, gate, up, act), gathered = fwd_layer(group_axis, hidden, *weights, following)
            saved.append((hidden, normed, gate, up, act, weights))
            hidden, weights = out, gathered
        h_out = hidden

        clock = 0.0
        chains = []
        parts = []

        def slot(anchor, spent):
            nonlocal clock, parts
            clock += spent
            parts = [c.step([anchor], clock) for c in chains if c.ready is not None and c.ready <= clock]

        downs, ups, gates = {}, {}, {}
        for layer in reversed(range(num_layers)):
            hidden, normed, gate, up, act, weights = saved[layer]
            orders = [tuple(AXIS_BITS[(layer + j + i) % 3] for i in range(3)) for j in range(3)]
            keep, send = dw_down_split(chip_table(orders[0]), act, fence(grad_in, parts))
            slot(keep, T_DOWN)
            downs[layer] = Chain(keep, send, orders[0], clock)
            chains.append(downs[layer])
            grad_new, d_gate, d_up = bwd_layer(hidden, fence(grad_in, [keep] + parts), gate, up, *weights)
            slot(d_up, T_BWD)
            d_up = fence(d_up, parts)
            full_up = dw_in(normed, d_up)
            ups[layer] = lax.psum_scatter(full_up, group_axis, scatter_dimension=0, tiled=True)
            slot(full_up, T_IN)
            d_gate = fence(d_gate, [full_up] + parts)
            ff = d_gate.shape[1]
            pieces = 3 if layer == 0 else 1
            gates[layer] = []
            for j in range(pieces):
                order = orders[(1 + j) % 3]
                table, cols = chip_table(order), ff // pieces
                keep, send = dw_in_split(table, normed, d_gate, j * cols, cols)
                slot(keep, T_IN / pieces)
                gates[layer].append(Chain(keep, send, order, clock))
                chains.append(gates[layer][-1])
                d_gate = fence(d_gate, [keep] + parts)
            grad_in = fence(grad_new, [keep] + parts)

        while any(c.ready is not None for c in chains):
            first = min((c for c in chains if c.ready is not None), key=lambda c: c.ready)
            clock = max(clock, first.ready)
            first.step([], clock)
        layers = range(num_layers)
        dw_gate = jnp.stack([jnp.concatenate([c.result for c in gates[i]], axis=-1) for i in layers])
        dw_up = jnp.stack([ups[i] for i in layers])
        dw_down = jnp.stack([downs[i].result for i in layers])
        return h_out.reshape(shape), grad_in.reshape(shape), dw_gate, dw_up, dw_down

    return jax.shard_map(
        local_step,
        mesh=mesh,
        in_specs=(token_spec, weight_spec, weight_spec, weight_spec, token_spec),
        out_specs=(token_spec, token_spec, weight_spec, weight_spec, weight_spec),
        check_vma=False,
    )
```

time: 1850 us -> 1560 us (0.84)
  Pallas kernels: 0 us -> 865 us
  matrix products: 845 us -> 0 us
  waiting for transfers between devices: 890 us -> 508 us
  other arithmetic: 50.6 us -> 116 us
  local copies, waits for them, and re-layouts: 41.8 us -> 11.7 us
  starting transfers between devices: 1.58 us -> 31.2 us
    pallas_call x0 -> x23, Pallas kernels: none -> 865 us  [the longest x4 281 us: fwd_layer(): pl.pallas_call(functools.partial(fwd_gather_kernel, axis) if more else fw...]
    dot_general x36 -> x0, matrix products: 845 us -> none  [the longest x4 165 us: block_bwd(): jnp.einsum('bsd,fd->bsf', grad_in, down_wt, preferred_element_type=jnp.fl...]
    reduce_scatter x12 -> x4, waiting for transfers between devices: 642 us -> 0.01 us  [local_step(): lax.psum_scatter(full_up, group_axis, scatter_dimension=0, tiled=True)]
    ppermute x0 -> x40, waiting for transfers between devices: none -> 508 us  [swap(): return lax.ppermute(value, group_axis, [(i, i ^ bit) for i in range(size)])]
    all_gather x12 -> x0, waiting for transfers between devices: 243 us -> none  [gather_layer(): lax.all_gather(w_stack[layer_idx], group_axis, axis=0, tiled=True)]
    add x0 -> x37, other arithmetic: none -> 107 us  [step(): total = total + arrived[low:high]]
    convert_element_type x4 -> x0, other arithmetic: 33.4 us -> none  [block_bwd(): new_grad = (grad_in.astype(jnp.float32) + d_hid).astype(jnp.bfloat16)]
    ppermute x0 -> x40, starting transfers between devices: none -> 31 us  [swap(): return lax.ppermute(value, group_axis, [(i, i ^ bit) for i in range(size)])]
  transfers between devices with their start and end apart: 24 -> 44, of which waited for: 19 -> 15; matrix products, arithmetic and copies ran while one was open for 44% -> 7% of each run, Pallas kernels for 0% -> 31%
where the time goes in v1:
time: 1560 us; the launch traced here: 1550 us
  Pallas kernels  865 us (55%)
  waiting for transfers between devices  508 us (33%)
  other arithmetic  116 us (7%)
  starting transfers between devices  31.2 us (2%)
    ppermute x40, waiting for transfers between devices, swap(): return lax.ppermute(value, group_axis, [(i, i ^ bit) for i in range(size)])  508 us
    pallas_call x4, Pallas kernels, fwd_layer(): pl.pallas_call(functools.partial(fwd_gather_kernel, axis) if more else fw...  281 us
    pallas_call x4, Pallas kernels, bwd_layer(): pl.pallas_call(bwd_kernel, grid=(nf, nm), in_specs=[pl.BlockSpec((TM, wid...  266 us
    add x37, other arithmetic, step(): total = total + arrived[low:high]  107 us
    pallas_call x6, Pallas kernels, dw_in_split(): pl.pallas_call(dw_in_split_kernel, grid_spec=pltpu.PrefetchScalarGridSpec...  92.1 us
    pallas_call x4, Pallas kernels, dw_down_split(): pl.pallas_call(dw_down_split_kernel, grid_spec=pltpu.PrefetchScalarGridSp...  80.8 us
    pallas_call x4, Pallas kernels, dw_in(): pl.pallas_call(dw_in_kernel, grid=(ff // TD,), in_specs=[pl.BlockSpec((to...  74.5 us
    pallas_call x1, Pallas kernels, gather_first(): pl.pallas_call(kernel, in_specs=[ANY] * 3, out_specs=[ANY] * 3, out_shape...  70.2 us
  transfers between devices with their start and end apart: 44, of which 15 were waited for; matrix products, arithmetic and copies ran while one was open for 7% of the time, Pallas kernels for 31%

profile of v1, /device:TPU:0, one launch (start us, length us, event | category | flops | bytes accessed | tf_op | source)
XLA Modules:
  0.0 1545.8 jit_solution(516319379378114128)
XLA Ops:
  11.6 70.2 %gather_first.1 = (bf16[2,2,2,2,64,3072]{5,4,3,2,1,0:T(8,128)(2,1)}, bf16[2,2,2,2,64,3072]{5,4,3,2,1,0:T(8,128)(2,1)}, bf16[2,2,2,2,192,1024]{5,4,3,2,1,0:T(8,128)(2,1)}) custom-call(bf16[64,3072]{1,0:T(8,128)(2,1)} %get-tuple-element.230.refs_0_, bf16[64,3072]{1,0:T(8,128)(2,1)} %get-tuple-element.223.refs_1_, bf16[192,1024]{1,0:T(8,128)(2,1)} %get-tuple-element.219.refs_2_), custom_call_target="tpu_custom_call" | custom-call | tf_op jit(solution)/shard_map/gather_first/pallas_call | solution.py:167
  81.9 75.8 %fwd_gather.3 = (bf16[2048,1024]{1,0:T(8,128)(2,1)}, bf16[2048,1024]{1,0:T(8,128)(2,1)}, f32[2048,3072]{1,0:T(8,128)}, f32[2048,3072]{1,0:T(8,128)}, bf16[2048,3...) custom-call(bf16[2048,1024]{1,0:T(8,128)(2,1)} %bitcast.75, ...), custom_call_target="tpu_custom_call" | custom-call | flops 38654705664 | bytes 75497472 | tf_op jit(solution)/shard_map/fwd_gather/pallas_call | solution.py:229
  157.7 75.7 %fwd_gather.4 = (bf16[2048,1024]{1,0:T(8,128)(2,1)}, bf16[2048,1024]{1,0:T(8,128)(2,1)}, f32[2048,3072]{1,0:T(8,128)}, f32[2048,3072]{1,0:T(8,128)}, bf16[2048,3...) custom-call(bf16[2048,1024]{1,0:T(8,128)(2,1)} %get-tuple-element.11, ...), custom_call_target="tpu_custom_call" | custom-call | flops 38654705664 | bytes 75497472 | tf_op jit(solution)/shard_map/fwd_gather/pallas_call | solution.py:229
  233.4 76.5 %fwd_gather.5 = (bf16[2048,1024]{1,0:T(8,128)(2,1)}, bf16[2048,1024]{1,0:T(8,128)(2,1)}, f32[2048,3072]{1,0:T(8,128)}, f32[2048,3072]{1,0:T(8,128)}, bf16[2048,3...) custom-call(bf16[2048,1024]{1,0:T(8,128)(2,1)} %get-tuple-element.11, ...), custom_call_target="tpu_custom_call" | custom-call | flops 38654705664 | bytes 75497472 | tf_op jit(solution)/shard_map/fwd_gather/pallas_call | solution.py:229
  309.8 52.8 %fwd_layer.1 = (bf16[2048,1024]{1,0:T(8,128)(2,1)}, bf16[2048,1024]{1,0:T(8,128)(2,1)}, f32[2048,3072]{1,0:T(8,128)}, f32[2048,3072]{1,0:T(8,128)}, bf16[2048,3072]{1,0:T(8,128)(2,1)}) custom-call(bf16[2048,1024]{1,0:T(8,128)(2,1)} %get-tuple-element.122.h_ref, bf16[1024,3072]{1,0:T(8,128)(2,1)} %bitcast.89, bf16[1024,3072]{1,0:T(8,128)(2,1)} %bitcast.91, ...), custom_call_target="tpu_custom_call" | custom-call | flops 38654705664 | bytes 75497472 | tf_op jit(solution)/shard_map/fwd_layer/pallas_call | solution.py:229
  363.3 20.0 %dw_down_split.4 = (f32[8,192,1024]{2,1,0:T(8,128)}, f32[8,192,1024]{2,1,0:T(8,128)}) custom-call(s32[9]{0:T(128)} %stack.49.block_of, bf16[2048,3072]{1,0:T(8,128)(2,1)} %get-tuple-element.127.act_ref, bf16[2048,1024]{1,0:T(8,128)(2,1)} %bitcast.73), custom_call_target="tpu_custom_call" | custom-call | flops 12884901888 | bytes 12582912 | tf_op jit(solution)/shard_map/dw_down_split/pallas_call | solution.py:410
  383.7 66.8 %bwd_layer.4 = (bf16[2048,1024]{1,0:T(8,128)(2,1)}, bf16[2048,3072]{1,0:T(8,128)(2,1)}, bf16[2048,3072]{1,0:T(8,128)(2,1)}) custom-call(bf16[2048,1024]{1,0:T(8,128)(2,1)} %get-tuple-element.122.h_ref, bf16[2048,1024]{1,0:T(8,128)(2,1)} %bitcast.74, f32[2048,3072]{1,0:T(8,128)} %get-tuple-element.130.gate_ref, f32[2048,3072]{1,0:T(8,128)} %get-tuple-element.131.up_ref, ...), custom_call_target="tpu_custom_call" | custom-call | flops 38654705664 | bytes 75497472 | tf_op jit(solution)/shard_map/bwd_layer/pallas_call | solution.py:310
  475.1 20.7 %dw_in_split.6 = (f32[8,64,3072]{2,1,0:T(8,128)}, f32[8,64,3072]{2,1,0:T(8,128)}) custom-call(s32[9]{0:T(128)} %stack.50.block_of, bf16[2048,1024]{1,0:T(8,128)(2,1)} %get-tuple-element.133.n_ref, bf16[2048,3072]{1,0:T(8,128)(2,1)} %get-tuple-element.139.d_ref), custom_call_target="tpu_custom_call" | custom-call | flops 12884901888 | bytes 12582912 | tf_op jit(solution)/shard_map/dw_in_split/pallas_call | solution.py:378
  496.5 20.8 %dw_down_split.5 = (f32[8,192,1024]{2,1,0:T(8,128)}, f32[8,192,1024]{2,1,0:T(8,128)}) custom-call(s32[9]{0:T(128)} %stack.51.block_of, bf16[2048,3072]{1,0:T(8,128)(2,1)} %get-tuple-element.142.act_ref, bf16[2048,1024]{1,0:T(8,128)(2,1)} %get-tuple-element.146.g_ref), custom_call_target="tpu_custom_call" | custom-call | flops 12884901888 | bytes 12582912 | tf_op jit(solution)/shard_map/dw_down_split/pallas_call | solution.py:410
  523.6 66.8 %bwd_layer.5 = (bf16[2048,1024]{1,0:T(8,128)(2,1)}, bf16[2048,3072]{1,0:T(8,128)(2,1)}, bf16[2048,3072]{1,0:T(8,128)(2,1)}) custom-call(bf16[2048,1024]{1,0:T(8,128)(2,1)} %get-tuple-element.118.refs_0_.h_ref, bf16[2048,1024]{1,0:T(8,128)(2,1)} %get-tuple-element.146.g_ref, f32[2048,3072]{1,0:T(8,128)} %get-tuple-element.147.gate_ref, ...), custom_call_target="tpu_custom_call" | custom-call | flops 38654705664 | bytes 75497472 | tf_op jit(solution)/shard_map/bwd_layer/pallas_call | solution.py:310
  590.5 26.0 %collective-permute-done.2 = f32[4,192,1024]{2,1,0:T(8,128)S(1)} collective-permute-done((f32[4,192,1024]{2,1,0:T(8,128)}, f32[4,192,1024]{2,1,0:T(8,128)S(1)}, u32[]{:S(2)}, u32[]{:S(2)}) %collective-permute-start.2) | collective-permute-done | bytes 3145760 | tf_op jit(solution)/shard_map/ppermute | solution.py:436
  644.4 20.4 %dw_in_split.7 = (f32[8,64,3072]{2,1,0:T(8,128)}, f32[8,64,3072]{2,1,0:T(8,128)}) custom-call(s32[9]{0:T(128)} %stack.49.block_of, bf16[2048,1024]{1,0:T(8,128)(2,1)} %get-tuple-element.150.n_ref, bf16[2048,3072]{1,0:T(8,128)(2,1)} %get-tuple-element.157.d_ref), custom_call_target="tpu_custom_call" | custom-call | flops 12884901888 | bytes 12582912 | tf_op jit(solution)/shard_map/dw_in_split/pallas_call | solution.py:378
  668.2 107.1 %collective-permute-done.4 = f32[4,64,3072]{2,1,0:T(8,128)S(1)} collective-permute-done((f32[4,64,3072]{2,1,0:T(8,128)}, f32[4,64,3072]{2,1,0:T(8,128)S(1)}, u32[]{:S(2)}, u32[]{:S(2)}) %collective-permute-start.4) | collective-permute-done | bytes 3145760 | tf_op jit(solution)/shard_map/ppermute | solution.py:436
  781.2 20.0 %dw_down_split.6 = (f32[8,192,1024]{2,1,0:T(8,128)}, f32[8,192,1024]{2,1,0:T(8,128)}) custom-call(s32[9]{0:T(128)} %stack.50.block_of, bf16[2048,3072]{1,0:T(8,128)(2,1)} %get-tuple-element.161.act_ref, bf16[2048,1024]{1,0:T(8,128)(2,1)} %get-tuple-element.167.g_ref), custom_call_target="tpu_custom_call" | custom-call | flops 12884901888 | bytes 12582912 | tf_op jit(solution)/shard_map/dw_down_split/pallas_call | solution.py:410
  818.1 66.3 %bwd_layer.6 = (bf16[2048,1024]{1,0:T(8,128)(2,1)}, bf16[2048,3072]{1,0:T(8,128)(2,1)}, bf16[2048,3072]{1,0:T(8,128)(2,1)}) custom-call(bf16[2048,1024]{1,0:T(8,128)(2,1)} %get-tuple-element.114.refs_0_.h_ref, bf16[2048,1024]{1,0:T(8,128)(2,1)} %get-tuple-element.167.g_ref, f32[2048,3072]{1,0:T(8,128)} %get-tuple-element.168.gate_ref, ...), custom_call_target="tpu_custom_call" | custom-call | flops 38654705664 | bytes 75497472 | tf_op jit(solution)/shard_map/bwd_layer/pallas_call | solution.py:310
  900.1 18.8 %dw_in.6 = f32[1024,3072]{1,0:T(8,128)} custom-call(bf16[2048,1024]{1,0:T(8,128)(2,1)} %get-tuple-element.171.n_ref, bf16[2048,3072]{1,0:T(8,128)(2,1)} %get-tuple-element.179.d_ref), custom_call_target="tpu_custom_call" | custom-call | flops 12884901888 | bytes 12582912 | tf_op jit(solution)/shard_map/dw_in/pallas_call | solution.py:351
  921.3 20.6 %dw_in_split.8 = (f32[8,64,3072]{2,1,0:T(8,128)}, f32[8,64,3072]{2,1,0:T(8,128)}) custom-call(s32[9]{0:T(128)} %stack.51.block_of, bf16[2048,1024]{1,0:T(8,128)(2,1)} %get-tuple-element.171.n_ref, bf16[2048,3072]{1,0:T(8,128)(2,1)} %get-tuple-element.180.d_ref), custom_call_target="tpu_custom_call" | custom-call | flops 12884901888 | bytes 12582912 | tf_op jit(solution)/shard_map/dw_in_split/pallas_call | solution.py:378
  944.0 104.0 %collective-permute-done.11 = f32[1,64,3072]{2,1,0:T(8,128)S(1)} collective-permute-done((f32[1,64,3072]{2,1,0:T(8,128)}, f32[1,64,3072]{2,1,0:T(8,128)S(1)}, u32[]{:S(2)}, u32[]{:S(2)}) %collective-permute-start.11) | collective-permute-done | bytes 786464 | tf_op jit(solution)/shard_map/ppermute | solution.py:436
  1053.8 20.0 %dw_down_split.7 = (f32[8,192,1024]{2,1,0:T(8,128)}, f32[8,192,1024]{2,1,0:T(8,128)}) custom-call(s32[9]{0:T(128)} %stack.49.block_of, bf16[2048,3072]{1,0:T(8,128)(2,1)} %get-tuple-element.185.act_ref, bf16[2048,1024]{1,0:T(8,128)(2,1)} %get-tuple-element.191.g_ref), custom_call_target="tpu_custom_call" | custom-call | flops 12884901888 | bytes 12582912 | tf_op jit(solution)/shard_map/dw_down_split/pallas_call | solution.py:410
  1089.6 66.3 %bwd_layer.7 = (bf16[2048,1024]{1,0:T(8,128)(2,1)}, bf16[2048,3072]{1,0:T(8,128)(2,1)}, bf16[2048,3072]{1,0:T(8,128)(2,1)}) custom-call(bf16[2048,1024]{1,0:T(8,128)(2,1)} %bitcast.76, bf16[2048,1024]{1,0:T(8,128)(2,1)} %get-tuple-element.191.g_ref, f32[2048,3072]{1,0:T(8,128)} %get-tuple-element.192.gate_ref, f32[2048,3072]{1,0:T(8,128)} %get-tuple-element.193.up_ref, ...), custom_call_target="tpu_custom_call" | custom-call | flops 38654705664 | bytes 75497472 | tf_op jit(solution)/shard_map/bwd_layer/pallas_call | solution.py:310
  1155.9 22.9 %collective-permute-done.16 = f32[2,64,3072]{2,1,0:T(8,128)S(1)} collective-permute-done((f32[2,64,3072]{2,1,0:T(8,128)}, f32[2,64,3072]{2,1,0:T(8,128)S(1)}, u32[]{:S(2)}, u32[]{:S(2)}) %collective-permute-start.16) | collective-permute-done | bytes 1572896 | tf_op jit(solution)/shard_map/ppermute | solution.py:436
  1263.1 126.2 %collective-permute-done.38 = f32[2,192,1024]{2,1,0:T(8,128)S(1)} collective-permute-done((f32[2,192,1024]{2,1,0:T(8,128)}, f32[2,192,1024]{2,1,0:T(8,128)S(1)}, u32[]{:S(2)}, u32[]{:S(2)}) %collective-permute-start.38) | collective-permute-done | bytes 1572896 | tf_op jit(solution)/shard_map/ppermute | solution.py:436
  1458.0 22.1 %collective-permute-done.27 = f32[2,64,1024]{2,1,0:T(8,128)S(1)} collective-permute-done((f32[2,64,1024]{2,1,0:T(8,128)S(1)}, f32[2,64,1024]{2,1,0:T(8,128)S(1)}, u32[]{:S(2)}, u32[]{:S(2)}) %collective-permute-start.27) | collective-permute-done | bytes 524320 | tf_op jit(solution)/shard_map/ppermute | solution.py:436
  1495.2 21.0 %collective-permute-done.24 = f32[1,64,1024]{2,1,0:T(8,128)S(1)} collective-permute-done((f32[1,64,1024]{2,1,0:T(8,128)S(1)}, f32[1,64,1024]{2,1,0:T(8,128)S(1)}, u32[]{:S(2)}, u32[]{:S(2)}) %collective-permute-start.24) | collective-permute-done | bytes 262176 | tf_op jit(solution)/shard_map/ppermute | solution.py:436
  (179 shorter events, 323.8 us)
Async XLA Ops:
  7.2 1528.1 %reduce-scatter.11.cloned.1.call-start = ((), (), s32[]{:S(2)}) async-start(), calls=%async_computation.7 | async-start | bytes 13369344 | tf_op jit(solution)/shard_map/reduce_scatter | solution.py:510
  474.4 1060.8 %reduce-scatter.9.cloned.1.call-start = ((), (), s32[]{:S(2)}) async-start(), calls=%async_computation.6 | async-start | bytes 13369344 | tf_op jit(solution)/shard_map/reduce_scatter | solution.py:510
  517.9 98.5 %collective-permute-start.2 = (f32[4,192,1024]{2,1,0:T(8,128)}, f32[4,192,1024]{2,1,0:T(8,128)S(1)}, u32[]{:S(2)}, u32[]{:S(2)}) collective-permute-start(f32[4,192,1024]{2,1,0:T(8,128)} %slice_add_fusion.6), channel_id=1, source_target_pairs={{0,2},{1,3},{2,0},{3,1},{4,6},{5,7},{6,4},{7,5},{8,10},{9,11},{10,... | collective-permute-start | bytes 9437192 | tf_op jit(solution)/shard_map/ppermute | solution.py:436
  644.3 890.9 %reduce-scatter.7.cloned.1.call-start = ((), (), s32[]{:S(2)}) async-start(), calls=%async_computation.5 | async-start | bytes 13369344 | tf_op jit(solution)/shard_map/reduce_scatter | solution.py:510
  664.7 148.4 %collective-permute-start.6 = (f32[8,64,3072]{2,1,0:T(8,128)}, f32[8,64,3072]{2,1,0:T(8,128)}, u32[]{:S(2)}, u32[]{:S(2)}) collective-permute-start(f32[8,64,3072]{2,1,0:T(8,128)} %get-tuple-element.165), channel_id=1, source_target_pairs={{0,1},{1,0},{2,3},{3,2},{4,5},{5,4},{6,7},{7,6},{8,9},{9,8},{10,11... | collective-permute-start | bytes 18874376 | tf_op jit(solution)/shard_map/ppermute | solution.py:436
  664.7 110.5 %collective-permute-start.4 = (f32[4,64,3072]{2,1,0:T(8,128)}, f32[4,64,3072]{2,1,0:T(8,128)S(1)}, u32[]{:S(2)}, u32[]{:S(2)}) collective-permute-start(f32[4,64,3072]{2,1,0:T(8,128)} %slice_add_fusion.5), channel_id=1, source_target_pairs={{0,4},{1,5},{2,6},{3,7},{4,0},{5,1},{6,2},{7,3},{8,12},{9,13},{10,... | collective-permute-start | bytes 9437192 | tf_op jit(solution)/shard_map/ppermute | solution.py:436
  666.1 142.4 %collective-permute-start.5 = (f32[2,192,1024]{2,1,0:T(8,128)}, f32[2,192,1024]{2,1,0:T(8,128)}, u32[]{:S(2)}, u32[]{:S(2)}) collective-permute-start(f32[2,192,1024]{2,1,0:T(8,128)} %slice_add_fusion.13), channel_id=1, source_target_pairs={{0,4},{1,5},{2,6},{3,7},{4,0},{5,1},{6,2},{7,3},{8,12},{9,13},{10,... | collective-permute-start | bytes 4718600 | tf_op jit(solution)/shard_map/ppermute | solution.py:436
  666.7 217.7 %collective-permute-start.9 = (f32[4,192,1024]{2,1,0:T(8,128)}, f32[4,192,1024]{2,1,0:T(8,128)S(1)}, u32[]{:S(2)}, u32[]{:S(2)}) collective-permute-start(f32[4,192,1024]{2,1,0:T(8,128)} %slice_add_fusion.4), channel_id=1, source_target_pairs={{0,8},{1,9},{2,10},{3,11},{4,12},{5,13},{6,14},{7,15},{8,0},{9,1},... | collective-permute-start | bytes 9437192 | tf_op jit(solution)/shard_map/ppermute | solution.py:436
  779.8 104.7 %collective-permute-start.8 = (f32[2,64,3072]{2,1,0:T(8,128)}, f32[2,64,3072]{2,1,0:T(8,128)}, u32[]{:S(2)}, u32[]{:S(2)}) collective-permute-start(f32[2,64,3072]{2,1,0:T(8,128)} %slice_add_fusion.12), channel_id=1, source_target_pairs={{0,8},{1,9},{2,10},{3,11},{4,12},{5,13},{6,14},{7,15},{8,0},{9,1},... | collective-permute-start | bytes 4718600 | tf_op jit(solution)/shard_map/ppermute | solution.py:436
  808.6 86.9 %collective-permute-start.10 = (f32[8,192,1024]{2,1,0:T(8,128)}, f32[8,192,1024]{2,1,0:T(8,128)}, u32[]{:S(2)}, u32[]{:S(2)}) collective-permute-start(f32[8,192,1024]{2,1,0:T(8,128)} %get-tuple-element.177), channel_id=1, source_target_pairs={{0,1},{1,0},{2,3},{3,2},{4,5},{5,4},{6,7},{7,6},{8,9},{9,8},{10,11... | collective-permute-start | bytes 18874376 | tf_op jit(solution)/shard_map/ppermute | solution.py:436
  918.9 616.3 %reduce-scatter.5.cloned.1.call-start = ((), (), s32[]{:S(2)}) async-start(), calls=%async_computation.4 | async-start | bytes 13369344 | tf_op jit(solution)/shard_map/reduce_scatter | solution.py:510
  920.8 127.2 %collective-permute-start.12 = (f32[4,64,3072]{2,1,0:T(8,128)S(1)}, f32[4,64,3072]{2,1,0:T(8,128)}, u32[]{:S(2)}, u32[]{:S(2)}) collective-permute-start(f32[4,64,3072]{2,1,0:T(8,128)S(1)} %copy-done.5), channel_id=1, source_target_pairs={{0,2},{1,3},{2,0},{3,1},{4,6},{5,7},{6,4},{7,5},{8,10},{9,11},{10,... | collective-permute-start | bytes 9437192 | tf_op jit(solution)/shard_map/ppermute | solution.py:436
  941.9 142.7 %collective-permute-start.14 = (f32[8,64,3072]{2,1,0:T(8,128)}, f32[8,64,3072]{2,1,0:T(8,128)}, u32[]{:S(2)}, u32[]{:S(2)}) collective-permute-start(f32[8,64,3072]{2,1,0:T(8,128)} %get-tuple-element.189), channel_id=1, source_target_pairs={{0,1},{1,0},{2,3},{3,2},{4,5},{5,4},{6,7},{7,6},{8,9},{9,8},{10,11... | collective-permute-start | bytes 18874376 | tf_op jit(solution)/shard_map/ppermute | solution.py:436
  941.9 106.0 %collective-permute-start.11 = (f32[1,64,3072]{2,1,0:T(8,128)}, f32[1,64,3072]{2,1,0:T(8,128)S(1)}, u32[]{:S(2)}, u32[]{:S(2)}) collective-permute-start(f32[1,64,3072]{2,1,0:T(8,128)} %slice_add_fusion.27), channel_id=1, source_target_pairs={{0,2},{1,3},{2,0},{3,1},{4,6},{5,7},{6,4},{7,5},{8,10},{9,11},{10,... | collective-permute-start | bytes 2359304 | tf_op jit(solution)/shard_map/ppermute | solution.py:436
  943.2 137.8 %collective-permute-start.13 = (f32[2,192,1024]{2,1,0:T(8,128)}, f32[2,192,1024]{2,1,0:T(8,128)}, u32[]{:S(2)}, u32[]{:S(2)}) collective-permute-start(f32[2,192,1024]{2,1,0:T(8,128)} %slice_add_fusion.11), channel_id=1, source_target_pairs={{0,2},{1,3},{2,0},{3,1},{4,6},{5,7},{6,4},{7,5},{8,10},{9,11},{10,... | collective-permute-start | bytes 4718600 | tf_op jit(solution)/shard_map/ppermute | solution.py:436
  1073.9 82.0 %collective-permute-start.17 = (f32[4,192,1024]{2,1,0:T(8,128)}, f32[4,192,1024]{2,1,0:T(8,128)}, u32[]{:S(2)}, u32[]{:S(2)}) collective-permute-start(f32[4,192,1024]{2,1,0:T(8,128)} %slice_add_fusion.2), channel_id=1, source_target_pairs={{0,4},{1,5},{2,6},{3,7},{4,0},{5,1},{6,2},{7,3},{8,12},{9,13},{10,... | collective-permute-start | bytes 9437192 | tf_op jit(solution)/shard_map/ppermute | solution.py:436
  1075.3 103.4 %collective-permute-start.16 = (f32[2,64,3072]{2,1,0:T(8,128)}, f32[2,64,3072]{2,1,0:T(8,128)S(1)}, u32[]{:S(2)}, u32[]{:S(2)}) collective-permute-start(f32[2,64,3072]{2,1,0:T(8,128)} %slice_add_fusion.10), channel_id=1, source_target_pairs={{0,4},{1,5},{2,6},{3,7},{4,0},{5,1},{6,2},{7,3},{8,12},{9,13},{10,... | collective-permute-start | bytes 4718600 | tf_op jit(solution)/shard_map/ppermute | solution.py:436
  1083.1 112.2 %collective-permute-start.15 = (f32[1,192,1024]{2,1,0:T(8,128)S(1)}, f32[1,192,1024]{2,1,0:T(8,128)}, u32[]{:S(2)}, u32[]{:S(2)}) collective-permute-start(f32[1,192,1024]{2,1,0:T(8,128)S(1)} %slice_add_fusion.26), channel_id=1, source_target_pairs={{0,4},{1,5},{2,6},{3,7},{4,0},{5,1},{6,2},{7,3},{8,12},{9,13},{10,... | collective-permute-start | bytes 2359304 | tf_op jit(solution)/shard_map/ppermute | solution.py:436
  1229.8 163.6 %collective-permute-start.35 = (f32[4,192,1024]{2,1,0:T(8,128)}, f32[4,192,1024]{2,1,0:T(8,128)}, u32[]{:S(2)}, u32[]{:S(2)}) collective-permute-start(f32[4,192,1024]{2,1,0:T(8,128)} %slice_add_fusion), channel_id=1, source_target_pairs={{0,2},{1,3},{2,0},{3,1},{4,6},{5,7},{6,4},{7,5},{8,10},{9,11},{10,... | collective-permute-start | bytes 9437192 | tf_op jit(solution)/shard_map/ppermute | solution.py:436
  1230.3 168.8 %collective-permute-start.20 = (f32[4,64,3072]{2,1,0:T(8,128)}, f32[4,64,3072]{2,1,0:T(8,128)}, u32[]{:S(2)}, u32[]{:S(2)}) collective-permute-start(f32[4,64,3072]{2,1,0:T(8,128)} %slice_add_fusion.1), channel_id=1, source_target_pairs={{0,8},{1,9},{2,10},{3,11},{4,12},{5,13},{6,14},{7,15},{8,0},{9,1},... | collective-permute-start | bytes 9437192 | tf_op jit(solution)/shard_map/ppermute | solution.py:436
  1262.6 126.7 %collective-permute-start.25 = (f32[8,64,1024]{2,1,0:T(8,128)}, f32[8,64,1024]{2,1,0:T(8,128)S(1)}, u32[]{:S(2)}, u32[]{:S(2)}) collective-permute-start(f32[8,64,1024]{2,1,0:T(8,128)} %get-tuple-element.215), channel_id=1, source_target_pairs={{0,1},{1,0},{2,3},{3,2},{4,5},{5,4},{6,7},{7,6},{8,9},{9,8},{10,11... | collective-permute-start | bytes 6291464 | tf_op jit(solution)/shard_map/ppermute | solution.py:436
  1262.6 126.7 %collective-permute-start.38 = (f32[2,192,1024]{2,1,0:T(8,128)}, f32[2,192,1024]{2,1,0:T(8,128)S(1)}, u32[]{:S(2)}, u32[]{:S(2)}) collective-permute-start(f32[2,192,1024]{2,1,0:T(8,128)} %slice_add_fusion.9), channel_id=1, source_target_pairs={{0,8},{1,9},{2,10},{3,11},{4,12},{5,13},{6,14},{7,15},{8,0},{9,1},... | collective-permute-start | bytes 4718600 | tf_op jit(solution)/shard_map/ppermute | solution.py:436
  1262.9 149.8 %collective-permute-start.21 = (f32[8,64,1024]{2,1,0:T(8,128)}, f32[8,64,1024]{2,1,0:T(8,128)}, u32[]{:S(2)}, u32[]{:S(2)}) collective-permute-start(f32[8,64,1024]{2,1,0:T(8,128)} %get-tuple-element.212), channel_id=1, source_target_pairs={{0,1},{1,0},{2,3},{3,2},{4,5},{5,4},{6,7},{7,6},{8,9},{9,8},{10,11... | collective-permute-start | bytes 6291464 | tf_op jit(solution)/shard_map/ppermute | solution.py:436
  1397.6 84.5 %collective-permute-start.36 = (f32[2,192,1024]{2,1,0:T(8,128)}, f32[2,192,1024]{2,1,0:T(8,128)}, u32[]{:S(2)}, u32[]{:S(2)}) collective-permute-start(f32[2,192,1024]{2,1,0:T(8,128)} %slice_add_fusion.7), channel_id=1, source_target_pairs={{0,4},{1,5},{2,6},{3,7},{4,0},{5,1},{6,2},{7,3},{8,12},{9,13},{10,... | collective-permute-start | bytes 4718600 | tf_op jit(solution)/shard_map/ppermute | solution.py:436
  (39 other events, 963.4 us)
Sparse Core Ops, SparseCore 0:
  474.6 120.2 reduce-scatter.10
  644.4 130.7 reduce-scatter.8
  919.0 129.9 reduce-scatter.6
  1228.8 129.9 reduce-scatter.4

commit v2 on v1

--- a/solution.py
+++ b/solution.py
@@ -13,14 +13,19 @@
 AXIS_BITS = (X, Y, Z)
 TM = 1024
 TF = 768
-SUB_FWD, SUB_BWD = 2, 4
+SUB_FWD, SUB_BWD = 2, 2
+TH = 512
 TD = 512
 VMEM_BYTES = 60 * 1024 * 1024
-FLIGHT, T_DOWN, T_BWD, T_IN = 95.0, 21.0, 66.0, 20.0
+FLIGHT, T_DOWN, T_HID, T_IN, T_OUT = 85.0, 21.0, 33.0, 20.0, 35.0
 
 
 def params(semantics):
     return pltpu.CompilerParams(dimension_semantics=semantics, vmem_limit_bytes=VMEM_BYTES)
+
+
+def dot_t(lhs, rhs):
+    return lax.dot_general(lhs, rhs, (((1,), (1,)), ((), ())), preferred_element_type=jnp.float32)
 
 
 def t_dot(lhs, rhs):
@@ -265,34 +270,53 @@
     return result[:5], flat(result[5:])
 
 
-def bwd_kernel(h_ref, g_ref, gate_ref, up_ref, wg_ref, wu_ref, wd_ref, out_ref, dgate_ref, dup_ref, acc, wg_t, wu_t, wd_t):
+def hidden_grad_kernel(g_ref, gate_ref, up_ref, wd_ref, dgate_ref, dup_ref):
+    m = pl.program_id(1)
+    size = TH // SUB_BWD
+    for sub in range(SUB_BWD):
+        here = pl.ds(sub * size, size)
+        there = pl.ds(pl.multiple_of(m * TH + sub * size, size), size)
+        d_act = dot_t(g_ref[there, :], wd_ref[...])
+        gate, up = gate_ref[here, :], up_ref[here, :]
+        sig = jax.nn.sigmoid(gate)
+        dgate_ref[here, :] = (d_act * up * (sig * (1.0 + gate * (1.0 - sig)))).astype(jnp.bfloat16)
+        dup_ref[here, :] = (d_act * (gate * sig)).astype(jnp.bfloat16)
+
+
+def hidden_grad(grad_in, gate, up, wd):
+    tokens, width = grad_in.shape
+    ff = wd.shape[0]
+    tile = pl.BlockSpec((TH, TF), lambda f, m: (m, f))
+    out = jax.ShapeDtypeStruct((tokens, ff), jnp.bfloat16)
+    return pl.pallas_call(
+        hidden_grad_kernel,
+        grid=(ff // TF, tokens // TH),
+        in_specs=[
+            pl.BlockSpec((tokens, width), lambda f, m: (0, 0)),
+            tile,
+            tile,
+            pl.BlockSpec((TF, width), lambda f, m: (f, 0)),
+        ],
+        out_specs=[tile, tile],
+        out_shape=[out, out],
+        compiler_params=params(("arbitrary", "arbitrary")),
+        cost_estimate=pl.CostEstimate(flops=2 * tokens * width * ff, bytes_accessed=12 * tokens * ff, transcendentals=0),
+        name="hidden_grad",
+    )(grad_in, gate, up, wd)
+
+
+def input_grad_kernel(h_ref, g_ref, dgate_ref, dup_ref, wg_ref, wu_ref, out_ref, acc):
     f, m = pl.program_id(0), pl.program_id(1)
     rows = pl.ds(pl.multiple_of(m * TM, TM), TM)
-
-    @pl.when(m == 0)
-    def _():
-        wd_t[...] = wd_ref[...].T
-        wg_t[...] = wg_ref[...].T
-        wu_t[...] = wu_ref[...].T
+    part = dot_t(dgate_ref[...], wg_ref[...]) + dot_t(dup_ref[...], wu_ref[...])
 
     @pl.when(f == 0)
     def _():
-        acc[rows, :] = jnp.zeros((TM, acc.shape[1]), jnp.float32)
-
-    for sub in range(SUB_BWD):
-        size = TM // SUB_BWD
-        here = pl.ds(sub * size, size)
-        there = pl.ds(pl.multiple_of(m * TM + sub * size, size), size)
-        d_act = jnp.dot(g_ref[here, :], wd_t[...], preferred_element_type=jnp.float32)
-        gate, up = gate_ref[here, :], up_ref[here, :]
-        sig = jax.nn.sigmoid(gate)
-        d_gate = (d_act * up * (sig * (1.0 + gate * (1.0 - sig)))).astype(jnp.bfloat16)
-        d_up = (d_act * (gate * sig)).astype(jnp.bfloat16)
-        dgate_ref[here, :] = d_gate
-        dup_ref[here, :] = d_up
-        acc[there, :] += jnp.dot(d_gate, wg_t[...], preferred_element_type=jnp.float32) + jnp.dot(
-            d_up, wu_t[...], preferred_element_type=jnp.float32
-        )
+        acc[rows, :] = part
+
+    @pl.when(f > 0)
+    def _():
+        acc[rows, :] += part
 
     @pl.when(f == pl.num_programs(0) - 1)
     def _():
@@ -303,42 +327,29 @@
         out_ref[...] = (g_ref[...].astype(jnp.float32) + d_hid).astype(jnp.bfloat16)
 
 
-def bwd_layer(hidden, grad_in, gate, up, wg, wu, wd):
+def input_grad(hidden, grad_in, d_gate, d_up, wg, wu):
     tokens, width = hidden.shape
     ff = wg.shape[1]
-    nf, nm = ff // TF, tokens // TM
+    nf = ff // TF
+    late = pl.BlockSpec((TM, width), lambda f, m: (jnp.where(f == nf - 1, m, 0), 0))
     return pl.pallas_call(
-        bwd_kernel,
-        grid=(nf, nm),
+        input_grad_kernel,
+        grid=(nf, tokens // TM),
         in_specs=[
-            pl.BlockSpec((TM, width), lambda f, m: (jnp.where(f == nf - 1, m, 0), 0)),
-            pl.BlockSpec((TM, width), lambda f, m: (m, 0)),
+            late,
+            late,
             pl.BlockSpec((TM, TF), lambda f, m: (m, f)),
             pl.BlockSpec((TM, TF), lambda f, m: (m, f)),
             pl.BlockSpec((width, TF), lambda f, m: (0, f)),
             pl.BlockSpec((width, TF), lambda f, m: (0, f)),
-            pl.BlockSpec((TF, width), lambda f, m: (f, 0)),
         ],
-        out_specs=[
-            pl.BlockSpec((TM, width), lambda f, m: (jnp.where(f == nf - 1, m, 0), 0)),
-            pl.BlockSpec((TM, TF), lambda f, m: (m, f)),
-            pl.BlockSpec((TM, TF), lambda f, m: (m, f)),
-        ],
-        out_shape=[
-            jax.ShapeDtypeStruct((tokens, width), jnp.bfloat16),
-            jax.ShapeDtypeStruct((tokens, ff), jnp.bfloat16),
-            jax.ShapeDtypeStruct((tokens, ff), jnp.bfloat16),
-        ],
-        scratch_shapes=[
-            pltpu.VMEM((tokens, width), jnp.float32),
-            pltpu.VMEM((TF, width), jnp.bfloat16),
-            pltpu.VMEM((TF, width), jnp.bfloat16),
-            pltpu.VMEM((width, TF), jnp.bfloat16),
-        ],
+        out_specs=late,
+        out_shape=jax.ShapeDtypeStruct((tokens, width), jnp.bfloat16),
+        scratch_shapes=[pltpu.VMEM((tokens, width), jnp.float32)],
         compiler_params=params(("arbitrary", "arbitrary")),
-        cost_estimate=pl.CostEstimate(flops=6 * tokens * width * ff, bytes_accessed=12 * tokens * ff, transcendentals=0),
-        name="bwd_layer",
-    )(hidden, grad_in, gate, up, wg, wu, wd)
+        cost_estimate=pl.CostEstimate(flops=4 * tokens * width * ff, bytes_accessed=8 * tokens * ff, transcendentals=0),
+        name="input_grad",
+    )(hidden, grad_in, d_gate, d_up, wg, wu)
 
 
 def dw_in_kernel(n_ref, d_ref, out_ref):
@@ -503,8 +514,8 @@
             slot(keep, T_DOWN)
             downs[layer] = Chain(keep, send, orders[0], clock)
             chains.append(downs[layer])
-            grad_new, d_gate, d_up = bwd_layer(hidden, fence(grad_in, [keep] + parts), gate, up, *weights)
-            slot(d_up, T_BWD)
+            d_gate, d_up = hidden_grad(fence(grad_in, [keep] + parts), gate, up, weights[2])
+            slot(d_up, T_HID)
             d_up = fence(d_up, parts)
             full_up = dw_in(normed, d_up)
             ups[layer] = lax.psum_scatter(full_up, group_axis, scatter_dimension=0, tiled=True)
@@ -521,7 +532,8 @@
                 gates[layer].append(Chain(keep, send, order, clock))
                 chains.append(gates[layer][-1])
                 d_gate = fence(d_gate, [keep] + parts)
-            grad_in = fence(grad_new, [keep] + parts)
+            grad_in = input_grad(hidden, grad_in, d_gate, d_up, *weights[:2])
+            slot(grad_in, T_OUT)
 
         while any(c.ready is not None for c in chains):
             first = min((c for c in chains if c.ready is not None), key=lambda c: c.ready)

time: 1560 us -> 1700 us (1.090)
  waiting for transfers between devices: 508 us -> 589 us
  Pallas kernels: 865 us -> 927 us
    ppermute x40, waiting for transfers between devices: 508 us -> 589 us  [swap(): return lax.ppermute(value, group_axis, [(i, i ^ bit) for i in range(size)])]
    pallas_call x4 -> x8, Pallas kernels: 266 us -> 321 us  [the longest x4 162 us: input_grad(): pl.pallas_call(input_grad_kernel, grid=(nf, tokens // TM), in_specs=[late...]
  transfers between devices with their start and end apart: 44 -> 44, of which waited for: 15 -> 15; matrix products, arithmetic and copies ran while one was open for 7% -> 7% of each run, Pallas kernels for 31% -> 32%
where the time goes in v2:
time: 1700 us; the launch traced here: 1690 us
  Pallas kernels  927 us (55%)
  waiting for transfers between devices  589 us (35%)
  other arithmetic  120 us (7%)
  starting transfers between devices  29.7 us (2%)
    ppermute x40, waiting for transfers between devices, swap(): return lax.ppermute(value, group_axis, [(i, i ^ bit) for i in range(size)])  589 us
    pallas_call x4, Pallas kernels, fwd_layer(): pl.pallas_call(functools.partial(fwd_gather_kernel, axis) if more else fw...  280 us
    pallas_call x4, Pallas kernels, input_grad(): pl.pallas_call(input_grad_kernel, grid=(nf, tokens // TM), in_specs=[late...  162 us
    pallas_call x4, Pallas kernels, hidden_grad(): pl.pallas_call(hidden_grad_kernel, grid=(ff // TF, tokens // TH), in_spec...  159 us
    add x37, other arithmetic, step(): total = total + arrived[low:high]  109 us
    pallas_call x6, Pallas kernels, dw_in_split(): pl.pallas_call(dw_in_split_kernel, grid_spec=pltpu.PrefetchScalarGridSpec...  101 us
    pallas_call x4, Pallas kernels, dw_down_split(): pl.pallas_call(dw_down_split_kernel, grid_spec=pltpu.PrefetchScalarGridSp...  80.1 us
    pallas_call x4, Pallas kernels, dw_in(): pl.pallas_call(dw_in_kernel, grid=(ff // TD,), in_specs=[pl.BlockSpec((to...  74 us
  transfers between devices with their start and end apart: 44, of which 15 were waited for; matrix products, arithmetic and copies ran while one was open for 7% of the time, Pallas kernels for 32%

profile of v2, /device:TPU:0, one launch (start us, length us, event | category | flops | bytes accessed | tf_op | source)
XLA Modules:
  0.0 1690.9 jit_solution(12517581856110436733)
XLA Ops:
  11.7 70.2 %gather_first.1 = (bf16[2,2,2,2,64,3072]{5,4,3,2,1,0:T(8,128)(2,1)}, bf16[2,2,2,2,64,3072]{5,4,3,2,1,0:T(8,128)(2,1)}, bf16[2,2,2,2,192,1024]{5,4,3,2,1,0:T(8,128)(2,1)}) custom-call(bf16[64,3072]{1,0:T(8,128)(2,1)} %get-tuple-element.236.refs_0_, bf16[64,3072]{1,0:T(8,128)(2,1)} %get-tuple-element.229.refs_1_, bf16[192,1024]{1,0:T(8,128)(2,1)} %get-tuple-element.225.refs_2_), custom_call_target="tpu_custom_call" | custom-call | tf_op jit(solution)/shard_map/gather_first/pallas_call | solution.py:172
  81.9 75.5 %fwd_gather.3 = (bf16[2048,1024]{1,0:T(8,128)(2,1)}, bf16[2048,1024]{1,0:T(8,128)(2,1)}, f32[2048,3072]{1,0:T(8,128)}, f32[2048,3072]{1,0:T(8,128)}, bf16[2048,3...) custom-call(bf16[2048,1024]{1,0:T(8,128)(2,1)} %bitcast.80, ...), custom_call_target="tpu_custom_call" | custom-call | flops 38654705664 | bytes 75497472 | tf_op jit(solution)/shard_map/fwd_gather/pallas_call | solution.py:234
  157.5 75.8 %fwd_gather.4 = (bf16[2048,1024]{1,0:T(8,128)(2,1)}, bf16[2048,1024]{1,0:T(8,128)(2,1)}, f32[2048,3072]{1,0:T(8,128)}, f32[2048,3072]{1,0:T(8,128)}, bf16[2048,3...) custom-call(bf16[2048,1024]{1,0:T(8,128)(2,1)} %get-tuple-element.11, ...), custom_call_target="tpu_custom_call" | custom-call | flops 38654705664 | bytes 75497472 | tf_op jit(solution)/shard_map/fwd_gather/pallas_call | solution.py:234
  233.2 76.2 %fwd_gather.5 = (bf16[2048,1024]{1,0:T(8,128)(2,1)}, bf16[2048,1024]{1,0:T(8,128)(2,1)}, f32[2048,3072]{1,0:T(8,128)}, f32[2048,3072]{1,0:T(8,128)}, bf16[2048,3...) custom-call(bf16[2048,1024]{1,0:T(8,128)(2,1)} %get-tuple-element.12, ...), custom_call_target="tpu_custom_call" | custom-call | flops 38654705664 | bytes 75497472 | tf_op jit(solution)/shard_map/fwd_gather/pallas_call | solution.py:234
  309.4 52.8 %fwd_layer.1 = (bf16[2048,1024]{1,0:T(8,128)(2,1)}, bf16[2048,1024]{1,0:T(8,128)(2,1)}, f32[2048,3072]{1,0:T(8,128)}, f32[2048,3072]{1,0:T(8,128)}, bf16[2048,3072]{1,0:T(8,128)(2,1)}) custom-call(bf16[2048,1024]{1,0:T(8,128)(2,1)} %get-tuple-element.125.h_ref, bf16[1024,3072]{1,0:T(8,128)(2,1)} %bitcast.90, bf16[1024,3072]{1,0:T(8,128)(2,1)} %bitcast.92, ...), custom_call_target="tpu_custom_call" | custom-call | flops 38654705664 | bytes 75497472 | tf_op jit(solution)/shard_map/fwd_layer/pallas_call | solution.py:234
  384.0 39.8 %hidden_grad.4 = (bf16[2048,3072]{1,0:T(8,128)(2,1)}, bf16[2048,3072]{1,0:T(8,128)(2,1)}) custom-call(bf16[2048,1024]{1,0:T(8,128)(2,1)} %bitcast.70, f32[2048,3072]{1,0:T(8,128)} %get-tuple-element.133.gate_ref, f32[2048,3072]{1,0:T(8,128)} %get-tuple-element.134.up_ref, bf16[3072,1024]{1,0:T(8,128)(2,1)} %bitcast.68), custom_call_target="tpu_custom_call" | custom-call | flops 12884901888 | bytes 75497472 | tf_op jit(solution)/shard_map/hidden_grad/pallas_call | solution.py:291
  447.8 30.0 %dw_in_split.6 = (f32[8,64,3072]{2,1,0:T(8,128)}, f32[8,64,3072]{2,1,0:T(8,128)}) custom-call(s32[9]{0:T(128)} %stack.50.block_of, bf16[2048,1024]{1,0:T(8,128)(2,1)} %get-tuple-element.136.n_ref, bf16[2048,3072]{1,0:T(8,128)(2,1)} %get-tuple-element.143.d_ref.dgate_ref), custom_call_target="tpu_custom_call" | custom-call | flops 12884901888 | bytes 12582912 | tf_op jit(solution)/shard_map/dw_in_split/pallas_call | solution.py:389
  478.6 40.9 %input_grad.4.g_ref = bf16[2048,1024]{1,0:T(8,128)(2,1)} custom-call(bf16[2048,1024]{1,0:T(8,128)(2,1)} %get-tuple-element.125.h_ref, bf16[2048,1024]{1,0:T(8,128)(2,1)} %bitcast.71, bf16[2048,3072]{1,0:T(8,128)(2,1)} %get-tuple-element.143.d_ref.dgate_ref, bf16[2048,3072]{1,0:T(8,128)(2,1)} %get-tuple-element.140.d_ref.dup_ref, ...), custom_call_target="tpu_custom_call" | custom-call | flops 25769803776 | bytes 50331648 | tf_op jit(solution)/shard_map/input_grad/pallas_call | solution.py:335
  545.6 69.8 %collective-permute-done.2 = f32[4,192,1024]{2,1,0:T(8,128)S(1)} collective-permute-done((f32[4,192,1024]{2,1,0:T(8,128)}, f32[4,192,1024]{2,1,0:T(8,128)S(1)}, u32[]{:S(2)}, u32[]{:S(2)}) %collective-permute-start.2) | collective-permute-done | bytes 3145760 | tf_op jit(solution)/shard_map/ppermute | solution.py:447
  622.1 39.7 %hidden_grad.5 = (bf16[2048,3072]{1,0:T(8,128)(2,1)}, bf16[2048,3072]{1,0:T(8,128)(2,1)}) custom-call(bf16[2048,1024]{1,0:T(8,128)(2,1)} %input_grad.4.g_ref, f32[2048,3072]{1,0:T(8,128)} %get-tuple-element.151.gate_ref, f32[2048,3072]{1,0:T(8,128)} %get-tuple-element.152.up_ref, bf16[3072,1024]{1,0:T(8,128)(2,1)} %bitcast.66), custom_call_target="tpu_custom_call" | custom-call | flops 12884901888 | bytes 75497472 | tf_op jit(solution)/shard_map/hidden_grad/pallas_call | solution.py:291
  731.7 40.3 %input_grad.5.g_ref = bf16[2048,1024]{1,0:T(8,128)(2,1)} custom-call(bf16[2048,1024]{1,0:T(8,128)(2,1)} %get-tuple-element.121.refs_0_.h_ref, bf16[2048,1024]{1,0:T(8,128)(2,1)} %input_grad.4.g_ref, bf16[2048,3072]{1,0:T(8,128)(2,1)} %get-tuple-element.163.d_ref.dgate_ref, bf16[2048,3072]{1,0:T(8,128)(2,1)} %get-tuple-element.158.d_ref.dup_ref, ...), custom_call_target="tpu_custom_call" | custom-call | flops 25769803776 | bytes 50331648 | tf_op jit(solution)/shard_map/input_grad/pallas_call | solution.py:335
  771.9 65.0 %collective-permute-done.6 = f32[1,192,1024]{2,1,0:T(8,128)} collective-permute-done((f32[1,192,1024]{2,1,0:T(8,128)}, f32[1,192,1024]{2,1,0:T(8,128)}, u32[]{:S(2)}, u32[]{:S(2)}) %collective-permute-start.6) | collective-permute-done | bytes 786464 | tf_op jit(solution)/shard_map/ppermute | solution.py:447
  865.7 36.7 %collective-permute-done.8 = f32[2,64,3072]{2,1,0:T(8,128)S(1)} collective-permute-done((f32[2,64,3072]{2,1,0:T(8,128)}, f32[2,64,3072]{2,1,0:T(8,128)S(1)}, u32[]{:S(2)}, u32[]{:S(2)}) %collective-permute-start.8) | collective-permute-done | bytes 1572896 | tf_op jit(solution)/shard_map/ppermute | solution.py:447
  911.8 40.0 %hidden_grad.6 = (bf16[2048,3072]{1,0:T(8,128)(2,1)}, bf16[2048,3072]{1,0:T(8,128)(2,1)}) custom-call(bf16[2048,1024]{1,0:T(8,128)(2,1)} %input_grad.5.g_ref, f32[2048,3072]{1,0:T(8,128)} %get-tuple-element.173.gate_ref, f32[2048,3072]{1,0:T(8,128)} %get-tuple-element.174.up_ref, bf16[3072,1024]{1,0:T(8,128)(2,1)} %bitcast.64), custom_call_target="tpu_custom_call" | custom-call | flops 12884901888 | bytes 75497472 | tf_op jit(solution)/shard_map/hidden_grad/pallas_call | solution.py:291
  1004.5 35.3 %collective-permute-done.13 = f32[4,64,3072]{2,1,0:T(8,128)} collective-permute-done((f32[4,64,3072]{2,1,0:T(8,128)}, f32[4,64,3072]{2,1,0:T(8,128)}, u32[]{:S(2)}, u32[]{:S(2)}) %collective-permute-start.13) | collective-permute-done | bytes 3145760 | tf_op jit(solution)/shard_map/ppermute | solution.py:447
  1042.4 40.5 %input_grad.6.g_ref = bf16[2048,1024]{1,0:T(8,128)(2,1)} custom-call(bf16[2048,1024]{1,0:T(8,128)(2,1)} %get-tuple-element.117.refs_0_.h_ref, bf16[2048,1024]{1,0:T(8,128)(2,1)} %input_grad.5.g_ref, bf16[2048,3072]{1,0:T(8,128)(2,1)} %get-tuple-element.186.d_ref.dgate_ref, bf16[2048,3072]{1,0:T(8,128)(2,1)} %get-tuple-element.181.d_ref.dup_ref, ...), custom_call_target="tpu_custom_call" | custom-call | flops 25769803776 | bytes 50331648 | tf_op jit(solution)/shard_map/input_grad/pallas_call | solution.py:335
  1082.9 46.5 %collective-permute-done.14 = f32[1,192,1024]{2,1,0:T(8,128)S(1)} collective-permute-done((f32[1,192,1024]{2,1,0:T(8,128)S(1)}, f32[1,192,1024]{2,1,0:T(8,128)S(1)}, u32[]{:S(2)}, u32[]{:S(2)}) %collective-permute-start.14) | collective-permute-done | bytes 786464 | tf_op jit(solution)/shard_map/ppermute | solution.py:447
  1157.8 35.6 %collective-permute-done.16 = f32[2,64,3072]{2,1,0:T(8,128)S(1)} collective-permute-done((f32[2,64,3072]{2,1,0:T(8,128)S(1)}, f32[2,64,3072]{2,1,0:T(8,128)S(1)}, u32[]{:S(2)}, u32[]{:S(2)}) %collective-permute-start.16) | collective-permute-done | bytes 1572896 | tf_op jit(solution)/shard_map/ppermute | solution.py:447
  1200.7 40.0 %hidden_grad.7 = (bf16[2048,3072]{1,0:T(8,128)(2,1)}, bf16[2048,3072]{1,0:T(8,128)(2,1)}) custom-call(bf16[2048,1024]{1,0:T(8,128)(2,1)} %input_grad.6.g_ref, f32[2048,3072]{1,0:T(8,128)} %get-tuple-element.196.gate_ref, f32[2048,3072]{1,0:T(8,128)} %get-tuple-element.197.up_ref, bf16[3072,1024]{1,0:T(8,128)(2,1)} %bitcast.62), custom_call_target="tpu_custom_call" | custom-call | flops 12884901888 | bytes 75497472 | tf_op jit(solution)/shard_map/hidden_grad/pallas_call | solution.py:291
  1269.9 140.6 %collective-permute-done.20 = f32[2,192,1024]{2,1,0:T(8,128)S(1)} collective-permute-done((f32[2,192,1024]{2,1,0:T(8,128)S(1)}, f32[2,192,1024]{2,1,0:T(8,128)S(1)}, u32[]{:S(2)}, u32[]{:S(2)}) %collective-permute-start.20) | collective-permute-done | bytes 1572896 | tf_op jit(solution)/shard_map/ppermute | solution.py:447
  1440.6 33.4 %collective-permute-done.34 = f32[2,64,3072]{2,1,0:T(8,128)S(1)} collective-permute-done((f32[2,64,3072]{2,1,0:T(8,128)S(1)}, f32[2,64,3072]{2,1,0:T(8,128)S(1)}, u32[]{:S(2)}, u32[]{:S(2)}) %collective-permute-start.34) | collective-permute-done | bytes 1572896 | tf_op jit(solution)/shard_map/ppermute | solution.py:447
  1493.7 62.2 %collective-permute-done.39 = f32[1,192,1024]{2,1,0:T(8,128)} collective-permute-done((f32[1,192,1024]{2,1,0:T(8,128)}, f32[1,192,1024]{2,1,0:T(8,128)}, u32[]{:S(2)}, u32[]{:S(2)}) %collective-permute-start.39) | collective-permute-done | bytes 786464 | tf_op jit(solution)/shard_map/ppermute | solution.py:447
  1556.0 40.1 %input_grad.7 = bf16[2048,1024]{1,0:T(8,128)(2,1)} custom-call(bf16[2048,1024]{1,0:T(8,128)(2,1)} %bitcast.81, bf16[2048,1024]{1,0:T(8,128)(2,1)} %input_grad.6.g_ref, bf16[2048,3072]{1,0:T(8,128)(2,1)} %get-tuple-element.217.d_ref.dgate_ref, bf16[2048,3072]{1,0:T(8,128)(2,1)} %get-tuple-element.204.d_ref.dup_ref, bf16[1024,3072]{1,0:T(8,128)(2,1)} %bitcast.77, ...), custom_call_target="tpu_custom_call" | custom-call | flops 25769803776 | bytes 50331648 | tf_op jit(solution)/shard_map/input_grad/pallas_call | solution.py:335
  1624.8 24.3 %collective-permute-done.29 = f32[1,64,1024]{2,1,0:T(8,128)S(1)} collective-permute-done((f32[1,64,1024]{2,1,0:T(8,128)S(1)}, f32[1,64,1024]{2,1,0:T(8,128)S(1)}, u32[]{:S(2)}, u32[]{:S(2)}) %collective-permute-start.29) | collective-permute-done | bytes 262176 | tf_op jit(solution)/shard_map/ppermute | solution.py:447
  (178 shorter events, 425.0 us)
Async XLA Ops:
  7.2 1672.9 %reduce-scatter.11.cloned.1.call-start = ((), (), s32[]{:S(2)}) async-start(), calls=%async_computation.7 | async-start | bytes 13369344 | tf_op jit(solution)/shard_map/reduce_scatter | solution.py:521
  447.7 1232.4 %reduce-scatter.9.cloned.1.call-start = ((), (), s32[]{:S(2)}) async-start(), calls=%async_computation.6 | async-start | bytes 13369344 | tf_op jit(solution)/shard_map/reduce_scatter | solution.py:521
  544.7 117.1 %collective-permute-start.3 = (f32[8,192,1024]{2,1,0:T(8,128)}, f32[8,192,1024]{2,1,0:T(8,128)}, u32[]{:S(2)}, u32[]{:S(2)}) collective-permute-start(f32[8,192,1024]{2,1,0:T(8,128)} %get-tuple-element.156), channel_id=1, source_target_pairs={{0,1},{1,0},{2,3},{3,2},{4,5},{5,4},{6,7},{7,6},{8,9},{9,8},{10,11... | collective-permute-start | bytes 18874376 | tf_op jit(solution)/shard_map/ppermute | solution.py:447
  545.0 70.5 %collective-permute-start.2 = (f32[4,192,1024]{2,1,0:T(8,128)}, f32[4,192,1024]{2,1,0:T(8,128)S(1)}, u32[]{:S(2)}, u32[]{:S(2)}) collective-permute-start(f32[4,192,1024]{2,1,0:T(8,128)} %slice_add_fusion.6), channel_id=1, source_target_pairs={{0,2},{1,3},{2,0},{3,1},{4,6},{5,7},{6,4},{7,5},{8,10},{9,11},{10,... | collective-permute-start | bytes 9437192 | tf_op jit(solution)/shard_map/ppermute | solution.py:447
  620.6 107.0 %collective-permute-start.5 = (f32[4,64,3072]{2,1,0:T(8,128)}, f32[4,64,3072]{2,1,0:T(8,128)}, u32[]{:S(2)}, u32[]{:S(2)}) collective-permute-start(f32[4,64,3072]{2,1,0:T(8,128)} %slice_add_fusion.5), channel_id=1, source_target_pairs={{0,4},{1,5},{2,6},{3,7},{4,0},{5,1},{6,2},{7,3},{8,12},{9,13},{10,... | collective-permute-start | bytes 9437192 | tf_op jit(solution)/shard_map/ppermute | solution.py:447
  685.8 994.3 %reduce-scatter.7.cloned.1.call-start = ((), (), s32[]{:S(2)}) async-start(), calls=%async_computation.5 | async-start | bytes 13369344 | tf_op jit(solution)/shard_map/reduce_scatter | solution.py:521
  710.0 130.4 %collective-permute-start.7 = (f32[8,64,3072]{2,1,0:T(8,128)}, f32[8,64,3072]{2,1,0:T(8,128)}, u32[]{:S(2)}, u32[]{:S(2)}) collective-permute-start(f32[8,64,3072]{2,1,0:T(8,128)} %get-tuple-element.166), channel_id=1, source_target_pairs={{0,1},{1,0},{2,3},{3,2},{4,5},{5,4},{6,7},{7,6},{8,9},{9,8},{10,11... | collective-permute-start | bytes 18874376 | tf_op jit(solution)/shard_map/ppermute | solution.py:447
  710.0 155.7 %collective-permute-start.9 = (f32[4,192,1024]{2,1,0:T(8,128)}, f32[4,192,1024]{2,1,0:T(8,128)S(1)}, u32[]{:S(2)}, u32[]{:S(2)}) collective-permute-start(f32[4,192,1024]{2,1,0:T(8,128)} %slice_add_fusion.4), channel_id=1, source_target_pairs={{0,8},{1,9},{2,10},{3,11},{4,12},{5,13},{6,14},{7,15},{8,0},{9,1},... | collective-permute-start | bytes 9437192 | tf_op jit(solution)/shard_map/ppermute | solution.py:447
  710.0 127.0 %collective-permute-start.6 = (f32[1,192,1024]{2,1,0:T(8,128)}, f32[1,192,1024]{2,1,0:T(8,128)}, u32[]{:S(2)}, u32[]{:S(2)}) collective-permute-start(f32[1,192,1024]{2,1,0:T(8,128)} %slice_add_fusion.27), channel_id=1, source_target_pairs={{0,8},{1,9},{2,10},{3,11},{4,12},{5,13},{6,14},{7,15},{8,0},{9,1},... | collective-permute-start | bytes 2359304 | tf_op jit(solution)/shard_map/ppermute | solution.py:447
  865.4 89.7 %collective-permute-start.11 = (f32[8,192,1024]{2,1,0:T(8,128)}, f32[8,192,1024]{2,1,0:T(8,128)}, u32[]{:S(2)}, u32[]{:S(2)}) collective-permute-start(f32[8,192,1024]{2,1,0:T(8,128)} %get-tuple-element.179), channel_id=1, source_target_pairs={{0,1},{1,0},{2,3},{3,2},{4,5},{5,4},{6,7},{7,6},{8,9},{9,8},{10,11... | collective-permute-start | bytes 18874376 | tf_op jit(solution)/shard_map/ppermute | solution.py:447
  909.8 69.3 %collective-permute-start.12 = (f32[2,192,1024]{2,1,0:T(8,128)}, f32[2,192,1024]{2,1,0:T(8,128)}, u32[]{:S(2)}, u32[]{:S(2)}) collective-permute-start(f32[2,192,1024]{2,1,0:T(8,128)} %slice_add_fusion.11), channel_id=1, source_target_pairs={{0,2},{1,3},{2,0},{3,1},{4,6},{5,7},{6,4},{7,5},{8,10},{9,11},{10,... | collective-permute-start | bytes 4718600 | tf_op jit(solution)/shard_map/ppermute | solution.py:447
  911.8 128.0 %collective-permute-start.13 = (f32[4,64,3072]{2,1,0:T(8,128)}, f32[4,64,3072]{2,1,0:T(8,128)}, u32[]{:S(2)}, u32[]{:S(2)}) collective-permute-start(f32[4,64,3072]{2,1,0:T(8,128)} %slice_add_fusion.3), channel_id=1, source_target_pairs={{0,2},{1,3},{2,0},{3,1},{4,6},{5,7},{6,4},{7,5},{8,10},{9,11},{10,... | collective-permute-start | bytes 9437192 | tf_op jit(solution)/shard_map/ppermute | solution.py:447
  979.2 700.9 %reduce-scatter.5.cloned.1.call-start = ((), (), s32[]{:S(2)}) async-start(), calls=%async_computation.4 | async-start | bytes 13369344 | tf_op jit(solution)/shard_map/reduce_scatter | solution.py:521
  1002.5 129.1 %collective-permute-start.15 = (f32[8,64,3072]{2,1,0:T(8,128)}, f32[8,64,3072]{2,1,0:T(8,128)}, u32[]{:S(2)}, u32[]{:S(2)}) collective-permute-start(f32[8,64,3072]{2,1,0:T(8,128)} %get-tuple-element.189), channel_id=1, source_target_pairs={{0,1},{1,0},{2,3},{3,2},{4,5},{5,4},{6,7},{7,6},{8,9},{9,8},{10,11... | collective-permute-start | bytes 18874376 | tf_op jit(solution)/shard_map/ppermute | solution.py:447
  1002.5 155.3 %collective-permute-start.17 = (f32[4,192,1024]{2,1,0:T(8,128)}, f32[4,192,1024]{2,1,0:T(8,128)}, u32[]{:S(2)}, u32[]{:S(2)}) collective-permute-start(f32[4,192,1024]{2,1,0:T(8,128)} %slice_add_fusion.2), channel_id=1, source_target_pairs={{0,4},{1,5},{2,6},{3,7},{4,0},{5,1},{6,2},{7,3},{8,12},{9,13},{10,... | collective-permute-start | bytes 9437192 | tf_op jit(solution)/shard_map/ppermute | solution.py:447
  1003.7 125.7 %collective-permute-start.14 = (f32[1,192,1024]{2,1,0:T(8,128)S(1)}, f32[1,192,1024]{2,1,0:T(8,128)S(1)}, u32[]{:S(2)}, u32[]{:S(2)}) collective-permute-start(f32[1,192,1024]{2,1,0:T(8,128)S(1)} %copy-done.15), channel_id=1, source_target_pairs={{0,4},{1,5},{2,6},{3,7},{4,0},{5,1},{6,2},{7,3},{8,12},{9,13},{10,... | collective-permute-start | bytes 2359304 | tf_op jit(solution)/shard_map/ppermute | solution.py:447
  1156.6 87.2 %collective-permute-start.19 = (f32[8,192,1024]{2,1,0:T(8,128)}, f32[8,192,1024]{2,1,0:T(8,128)}, u32[]{:S(2)}, u32[]{:S(2)}) collective-permute-start(f32[8,192,1024]{2,1,0:T(8,128)} %get-tuple-element.202), channel_id=1, source_target_pairs={{0,1},{1,0},{2,3},{3,2},{4,5},{5,4},{6,7},{7,6},{8,9},{9,8},{10,11... | collective-permute-start | bytes 18874376 | tf_op jit(solution)/shard_map/ppermute | solution.py:447
  1267.8 166.2 %collective-permute-start.21 = (f32[4,64,3072]{2,1,0:T(8,128)}, f32[4,64,3072]{2,1,0:T(8,128)}, u32[]{:S(2)}, u32[]{:S(2)}) collective-permute-start(f32[4,64,3072]{2,1,0:T(8,128)} %slice_add_fusion.1), channel_id=1, source_target_pairs={{0,8},{1,9},{2,10},{3,11},{4,12},{5,13},{6,14},{7,15},{8,0},{9,1},... | collective-permute-start | bytes 9437192 | tf_op jit(solution)/shard_map/ppermute | solution.py:447
  1268.7 141.8 %collective-permute-start.20 = (f32[2,192,1024]{2,1,0:T(8,128)S(1)}, f32[2,192,1024]{2,1,0:T(8,128)S(1)}, u32[]{:S(2)}, u32[]{:S(2)}) collective-permute-start(f32[2,192,1024]{2,1,0:T(8,128)S(1)} %slice_add_fusion.9), channel_id=1, source_target_pairs={{0,8},{1,9},{2,10},{3,11},{4,12},{5,13},{6,14},{7,15},{8,0},{9,1},... | collective-permute-start | bytes 4718600 | tf_op jit(solution)/shard_map/ppermute | solution.py:447
  1438.6 165.9 %collective-permute-start.36 = (f32[4,192,1024]{2,1,0:T(8,128)}, f32[4,192,1024]{2,1,0:T(8,128)}, u32[]{:S(2)}, u32[]{:S(2)}) collective-permute-start(f32[4,192,1024]{2,1,0:T(8,128)} %slice_add_fusion), channel_id=1, source_target_pairs={{0,2},{1,3},{2,0},{3,1},{4,6},{5,7},{6,4},{7,5},{8,10},{9,11},{10,... | collective-permute-start | bytes 9437192 | tf_op jit(solution)/shard_map/ppermute | solution.py:447
  1439.3 116.6 %collective-permute-start.39 = (f32[1,192,1024]{2,1,0:T(8,128)}, f32[1,192,1024]{2,1,0:T(8,128)}, u32[]{:S(2)}, u32[]{:S(2)}) collective-permute-start(f32[1,192,1024]{2,1,0:T(8,128)} %slice_add_fusion.23), channel_id=1, source_target_pairs={{0,2},{1,3},{2,0},{3,1},{4,6},{5,7},{6,4},{7,5},{8,10},{9,11},{10,... | collective-permute-start | bytes 2359304 | tf_op jit(solution)/shard_map/ppermute | solution.py:447
  1476.7 122.0 %collective-permute-start.35 = (f32[1,64,3072]{2,1,0:T(8,128)}, f32[1,64,3072]{2,1,0:T(8,128)}, u32[]{:S(2)}, u32[]{:S(2)}) collective-permute-start(f32[1,64,3072]{2,1,0:T(8,128)} %slice_add_fusion.21), channel_id=1, source_target_pairs={{0,4},{1,5},{2,6},{3,7},{4,0},{5,1},{6,2},{7,3},{8,12},{9,13},{10,... | collective-permute-start | bytes 2359304 | tf_op jit(solution)/shard_map/ppermute | solution.py:447
  1479.1 119.7 %collective-permute-start.24 = (f32[4,64,1024]{2,1,0:T(8,128)}, f32[4,64,1024]{2,1,0:T(8,128)}, u32[]{:S(2)}, u32[]{:S(2)}) collective-permute-start(f32[4,64,1024]{2,1,0:T(8,128)} %slice_add_fusion.16), channel_id=1, source_target_pairs={{0,4},{1,5},{2,6},{3,7},{4,0},{5,1},{6,2},{7,3},{8,12},{9,13},{10,... | collective-permute-start | bytes 3145736 | tf_op jit(solution)/shard_map/ppermute | solution.py:447
  1492.9 108.4 %collective-permute-start.27 = (f32[4,64,1024]{2,1,0:T(8,128)}, f32[4,64,1024]{2,1,0:T(8,128)}, u32[]{:S(2)}, u32[]{:S(2)}) collective-permute-start(f32[4,64,1024]{2,1,0:T(8,128)} %slice_add_fusion.15), channel_id=1, source_target_pairs={{0,8},{1,9},{2,10},{3,11},{4,12},{5,13},{6,14},{7,15},{8,0},{9,1},... | collective-permute-start | bytes 3145736 | tf_op jit(solution)/shard_map/ppermute | solution.py:447
  (37 other events, 996.1 us)
Sparse Core Ops, SparseCore 0:
  447.8 90.4 reduce-scatter.10
  685.9 129.7 reduce-scatter.8
  979.3 130.6 reduce-scatter.6
  1267.9 130.6 reduce-scatter.4
